TPU v7x, 32 devices: a 4x4x1 block of a 4x4x8 slice. The times are simulated.
32 devices in a mesh: dp: 1 (over z), tp: 4 (over y), sp: 8 (over x, core).
Axes of the slice: x: 4, y: 4, z: 1, core: 2. Of those that a mesh axis runs over, the one named last changes fastest.
The devices are a block of a 4x4x8 slice.
Arguments:
- x_in: bfloat16 [131072, 384], P(('dp', 'sp'))
- grad_y: bfloat16 [131072, 384], P(('dp', 'sp'))
- w_qkv: bfloat16 [384, 3, 384], P(None, None, 'tp')
- w_out: bfloat16 [384, 384], P('tp')
- ln_gamma: float32 [384], replicated
- ln_beta: float32 [384], replicated
- temperature: float32 [8], replicated
Outputs:
- output 1: bfloat16 [131072, 384], P(('dp', 'sp'))
- output 2: bfloat16 [131072, 384], P(('dp', 'sp'))
- output 3: float32 [384, 3, 384], P(('dp', 'sp'), None, 'tp')
- output 4: float32 [384, 384], P(('dp', 'tp', 'sp'))
- output 5: float32 [384], P('dp')
- output 6: float32 [384], P('dp')
- output 7: float32 [8], P('dp')
All inputs are finite; a program needn't handle non-finite values.
Results may differ from a plain program's by a relative error of at most 0.001.
Values are sent between devices in bfloat16 or wider.
A program may use at most 768 MiB of HBM per device.

v0:
```python
import jax
import jax.numpy as jnp
from jax import lax
from jax.sharding import PartitionSpec as P

LN_EPS = 1e-6


def layer_norm_fwd(x_rows, ln_gamma, ln_beta):
    x_float = x_rows.astype(jnp.float32)
    centered = x_float - jnp.mean(x_float, axis=-1, keepdims=True)
    inv_std = lax.rsqrt(jnp.mean(centered * centered, axis=-1, keepdims=True) + LN_EPS)
    x_hat = centered * inv_std
    return x_hat, inv_std, (x_hat * ln_gamma + ln_beta).astype(jnp.bfloat16)


def layer_norm_bwd(grad_u, x_hat, inv_std, ln_gamma):
    value_a9 = grad_u * ln_gamma
    return inv_std * (value_a9 - jnp.mean(value_a9, axis=-1, keepdims=True) - x_hat * jnp.mean(value_a9 * x_hat, axis=-1, keepdims=True))


def state_forward(gram_mat, q_sq, k_sq, temp_heads):
    norm_prod = jnp.sqrt(q_sq)[:, :, None] * jnp.sqrt(k_sq)[:, None, :]
    gram_n = gram_mat / norm_prod
    attn_prob = jax.nn.softmax(temp_heads[:, None, None] * gram_n, axis=-1)
    return gram_n, norm_prod, attn_prob


def state_backward(d_attn, attn_prob, gram_n, norm_prod, q_sq, k_sq, temp_heads):
    d_logit = attn_prob * (d_attn - jnp.sum(attn_prob * d_attn, axis=-1, keepdims=True))
    temp_grad = jnp.sum(d_logit * gram_n, axis=(1, 2))
    grad_sn = temp_heads[:, None, None] * d_logit
    d_gram = (grad_sn / norm_prod).astype(jnp.bfloat16)
    prod_sn = grad_sn * gram_n
    q_coef = -jnp.sum(prod_sn, axis=2) / q_sq
    k_coef = -jnp.sum(prod_sn, axis=1) / k_sq
    return d_gram, q_coef, k_coef, temp_grad


def solution(mesh):
    tp_size = mesh.shape["tp"]
    row_spec = P(("dp", "sp"), None)

    def local_step(x_blk, grad_blk, w_qkv, w_out, ln_gamma, ln_beta, value_a11):
        tokens, model_width = x_blk.shape
        local_cols = w_qkv.shape[2]
        heads_loc = value_a11.shape[0] // tp_size
        head_dim = local_cols // heads_loc
        temp_heads = lax.dynamic_slice_in_dim(value_a11, lax.axis_index("tp") * heads_loc, heads_loc)
        x_hat, inv_std, u_act = layer_norm_fwd(x_blk, ln_gamma, ln_beta)
        qkv_act = jnp.einsum("nd,dec->nec", u_act, w_qkv, preferred_element_type=jnp.float32).astype(jnp.bfloat16)
        qkv_heads = qkv_act.reshape(tokens, 3, heads_loc, head_dim)
        q_act = qkv_heads[:, 0]
        k_act = qkv_heads[:, 1]
        v_act = qkv_heads[:, 2]
        gram_part = jnp.einsum("nhi,nhj->hij", q_act, k_act, preferred_element_type=jnp.float32)
        q_part = jnp.einsum("nhi,nhi->hi", q_act, q_act, preferred_element_type=jnp.float32)
        k_part = jnp.einsum("nhj,nhj->hj", k_act, k_act, preferred_element_type=jnp.float32)
        gram_mat, q_sq, k_sq = lax.psum((gram_part, q_part, k_part), "sp")
        gram_n, norm_prod, attn_prob = state_forward(gram_mat, q_sq, k_sq, temp_heads)
        attn_bf = attn_prob.astype(jnp.bfloat16)
        out_act = jnp.einsum("hij,nhj->nhi", attn_bf, v_act, preferred_element_type=jnp.float32).astype(jnp.bfloat16)
        w_out_heads = w_out.reshape(heads_loc, head_dim, model_width)
        y_part = jnp.einsum("nhi,hid->nd", out_act, w_out_heads, preferred_element_type=jnp.float32)
        y_out = (x_blk.astype(jnp.float32) + lax.psum(y_part, "tp")).astype(jnp.bfloat16)
        wout_part = jnp.einsum("nhi,nd->hid", out_act, grad_blk, preferred_element_type=jnp.float32).reshape(local_cols, model_width)
        grad_wout = lax.psum_scatter(wout_part, "sp", scatter_dimension=0, tiled=True)
        dout_act = jnp.einsum("nd,hid->nhi", grad_blk, w_out_heads, preferred_element_type=jnp.float32).astype(jnp.bfloat16)
        d_attn = lax.psum(jnp.einsum("nhi,nhj->hij", dout_act, v_act, preferred_element_type=jnp.float32), "sp")
        dv_act = jnp.einsum("hij,nhi->nhj", attn_bf, dout_act, preferred_element_type=jnp.float32).astype(jnp.bfloat16)
        d_gram, q_coef, k_coef, temp_grad = state_backward(d_attn, attn_prob, gram_n, norm_prod, q_sq, k_sq, temp_heads)
        dq_act = (jnp.einsum("hij,nhj->nhi", d_gram, k_act, preferred_element_type=jnp.float32) + q_act * q_coef).astype(jnp.bfloat16)
        dk_act = (jnp.einsum("hij,nhi->nhj", d_gram, q_act, preferred_element_type=jnp.float32) + k_act * k_coef).astype(jnp.bfloat16)
        dqkv_act = jnp.stack([dq_act, dk_act, dv_act], axis=1).reshape(tokens, 3, local_cols)
        wqkv_part = jnp.einsum("nd,nec->dec", u_act, dqkv_act, preferred_element_type=jnp.float32)
        grad_wqkv = lax.psum_scatter(wqkv_part, "sp", scatter_dimension=0, tiled=True)
        grad_u = lax.psum(jnp.einsum("nec,dec->nd", dqkv_act, w_qkv, preferred_element_type=jnp.float32), "tp")
        grad_gamma, grad_beta = lax.psum((jnp.sum(grad_u * x_hat, axis=0), jnp.sum(grad_u, axis=0)), "sp")
        grad_x = (grad_blk.astype(jnp.float32) + layer_norm_bwd(grad_u, x_hat, inv_std, ln_gamma)).astype(jnp.bfloat16)
        grad_temp = lax.all_gather(temp_grad, "tp", tiled=True)
        return y_out, grad_x, grad_wqkv, grad_wout, grad_gamma, grad_beta, grad_temp

    in_specs = (row_spec, row_spec, P(None, None, "tp"), P("tp", None), P(None), P(None), P(None))
    out_specs = (row_spec, row_spec, P(("dp", "sp"), None, "tp"), P(("dp", "tp", "sp"), None), P("dp"), P("dp"), P("dp"))
    return jax.shard_map(local_step, mesh=mesh, in_specs=in_specs, out_specs=out_specs, check_vma=False)
```

profile of v0, /device:TPU:97, one launch (start us, length us, event | category | flops | bytes accessed | tf_op | source)
XLA Modules:
  0.0 1026.0 jit_solution(6609268678643268684)
XLA Ops:
  8.0 0.0 copy-start
  8.1 0.1 all-reduce.8.cloned.1.call-start
  8.1 0.0 copy-start.2
  8.1 8.2 convert_reduce_fusion
  16.4 0.0 copy-start.5
  16.4 0.0 copy-start.9
  16.4 0.1 copy-done.2
  16.5 6.5 fusion.17
  23.1 0.0 copy-done
  23.1 0.0 copy-done.5
  23.1 0.0 copy-done.9
  23.1 6.7 fusion.74
  29.9 1.0 convert_element_type.54
  30.9 0.0 copy-start.3
  30.9 2.6 fusion.30
  33.5 1.2 copy-done.3
  34.6 0.9 fusion.32
  35.6 8.5 convolution_convert_fusion.2
  44.1 3.5 fusion.36
  47.6 26.5 %all-reduce.4 = (f32[2,48,48]{2,1,0:T(8,128)}, f32[2,48]{1,0:T(2,128)}, f32[2,48]{1,0:T(2,128)}, f32[2,48,48]{2,1,0:T(8,128)}) all-reduce(f32[2,48,48]{2,1,0:T(8,128)S(1)} %fusion.32, f32[2,48]{1,0:T(2,128)} %get-tuple-element.12, f32[2,48]{1,0:T(2,128)S(1)} %get-tuple-element.11, ...), channel_id=1, replica_groups=mesh['dp'=1,'tp'=4,'sp'=8] {'sp'}, use_global_device_ids=true, to_apply=%region_2.0 | all-reduce | flops 9408 | bytes 75264 | tf_op jit(solution)/shard_map/psum | solution.py:59
  74.1 0.8 sqrt.7
  74.8 0.7 sqrt.6
  75.5 0.7 dynamic_slice.3
  76.3 1.6 fusion.76
  77.9 3.6 convolution_convert_fusion.1
  81.5 3.0 fusion.23
  84.5 1.3 fusion.52
  85.8 0.0 copy-done.6
  85.8 0.0 copy-done.7
  85.9 5.8 fusion.21
  91.7 5.9 fusion.22
  97.6 11.1 %convolution_bitcast_fusion = f32[16384,384]{1,0:T(8,128)} fusion(bf16[16384,2,48]{0,2,1:T(8,128)(2,1)S(1)} %fusion.23, bf16[2,48,384]{2,1,0:T(8,128)(2,1)} %bitcast.86), kind=kOutput, calls=%fused_computation.21 | convolution fusion | flops 1207959552 | bytes 28385280 | tf_op jit(solution)/shard_map/nhi,hid->nd/dot_general | solution.py:64
  108.7 0.0 copy-done.4
  108.7 0.0 copy-done.11
  108.7 0.0 copy-done.12
  108.7 12.2 %convolution_bitcast_fusion.1 = f32[16384,384]{1,0:T(8,128)} fusion(bf16[384,3,96]{0,2,1:T(8,128)(2,1)S(1)} %copy-done, bf16[16384,1,96]{0,2,1:T(8,128)(2,1)S(1)} %bitcast.83, bf16[16384,1,96]{0,2,1:T(8,128)(2,1)S(1)} %bitcast.88, bf16[16384,1,96]{0,2,1:T(8,128)(2,1)S(1)} %bitcast.90), kind=kOutput, calls=%fused_computation.22 | convolution fusion | flops 3633315840 | bytes 34824192 | tf_op jit(solution)/shard_map/nec,dec->nd/dot_general | solution.py:77
  120.9 0.1 all-reduce.8.cloned.1.call-update
  121.0 0.0 copy-start.10
  121.0 0.1 reduce-scatter.4.cloned.1.call-start
  121.0 6.8 fusion.26
  127.9 17.1 %fusion = f32[16,384]{1,0:T(8,128)S(1)} fusion(f32[96,384]{1,0:T(8,128)S(1)} %bitcast.84), kind=kCustom, calls=%all-reduce-scatter | all-reduce-scatter fusion | flops 49153 | bytes 172544
  145.0 2.0 collective-permute-start
  146.9 0.0 copy-start.13
  147.0 0.0 copy-start.8
  147.0 1.3 collective-permute-start.1
  148.3 0.0 copy-done.10
  148.3 16.4 %fusion.24 = f32[384,3,96]{2,0,1:T(8,128)} fusion(bf16[16384,1,96]{0,2,1:T(8,128)(2,1)} %bitcast.82, bf16[16384,1,96]{0,2,1:T(8,128)(2,1)} %bitcast.87, bf16[16384,1,96]{0,2,1:T(8,128)(2,1)} %bitcast.89, bf16[16384,384]{1,0:T(8,128)(2,1)} %param.7, f32[384]{0:T(512)S(1)} %copy-done.10, f32[384]{0:T(512)S(1)} %copy-done.5, f32[16384]{0:T(1024)S(1)} %add_rsqrt_fusion, ...), kind=kOutput, calls=%fused_computation.34 | convolution fusion | flops 3689938944 | bytes 22596608 | tf_op jit(solution)/shard_map/nd,nec->dec/dot_general | solution.py:75
  164.7 0.0 copy-done.13
  164.7 0.6 dynamic-slice
  166.0 0.2 dynamic-update-slice
  166.2 0.1 reduce-scatter.4.cloned.1.call-update
  166.3 11.9 %all-reduce = f32[8]{0:T(128)} all-reduce(f32[8]{0:T(128)S(1)} %dynamic-update-slice), channel_id=1, replica_groups=mesh['dp'=1,'tp'=4,'sp'=8] {'tp'}, use_global_device_ids=true, to_apply=%add | all-reduce | flops 8 | bytes 64
  178.1 0.0 copy-done.8
  178.1 0.6 dynamic-slice.5
  179.4 0.0 collective-permute-done.1
  179.4 0.0 collective-permute-done
  179.4 0.3 concatenate.1
  179.7 0.6 constant_dynamic-slice_fusion
  180.3 774.3 %all-reduce.8.cloned.1.call-done = (f32[16384,384]{1,0:T(8,128)}, f32[16384,384]{1,0:T(8,128)}) async-done(((f32[16384,384]{1,0:T(8,128)}, f32[16384,384]{1,0:T(8,128)}), (f32[16384,384]{1,0:T(8,128)}, f32[16384,384]{1,0:T(8,128)})) %all-reduce.8.cloned.1.call-update) | async-done | bytes 50331664 | tf_op jit(solution)/shard_map/psum | solution.py:65
  954.6 17.8 %fusion.16 = (f32[384]{0:T(512)S(1)}, f32[16384]{0:T(1024)S(1)}, f32[16384]{0:T(1024)S(1)}, f32[384]{0:T(512)S(1)}) fusion(f32[16384,384]{1,0:T(8,128)} %get-tuple-element.23, bf16[16384,384]{1,0:T(8,128)(2,1)} %param.7, f32[16384]{0:T(1024)S(1)} %add_rsqrt_fusion, f32[16384]{0:T(1024)S(1)} %broadcast_multiply_fusion.2, f32[384]{0:T(512)S(1)} %copy-done.5), kind=kLoop, calls=%fused_computation.18 | loop fusion | flops 62881024 | bytes 38015488 | tf_op jit(solution)/shard_map/reduce_sum | solution.py:78
  972.4 0.0 copy-start.1
  972.4 32.7 %fusion.15 = (bf16[16384,384]{1,0:T(8,128)(2,1)}, bf16[16384,384]{1,0:T(8,128)(2,1)}) fusion(bf16[16384,384]{1,0:T(8,128)(2,1)} %param.7, bf16[16384,384]{1,0:T(8,128)(2,1)} %param.8, f32[16384,384]{1,0:T(8,128)} %get-tuple-element.23, f32[16384]{0:T(1024)S(1)} %broadcast_multiply_fusion, f32[16384]{0:T(1024)S(1)} %broadcast_multiply_fusion.1, ...), kind=kLoop, calls=%fused_computation.17 | loop fusion | flops 81788928 | bytes 100926976 | tf_op jit(solution)/shard_map/convert_element_type | solution.py:79
  1005.2 13.3 %all-reduce.3 = (f32[384]{0:T(512)}, f32[384]{0:T(512)}) all-reduce(f32[384]{0:T(512)S(1)} %get-tuple-element.7, f32[384]{0:T(512)S(1)} %get-tuple-element.10), channel_id=1, replica_groups=mesh['dp'=1,'tp'=4,'sp'=8] {'sp'}, use_global_device_ids=true, to_apply=%region_18.0 | all-reduce | flops 768 | bytes 6144 | tf_op jit(solution)/shard_map/psum | solution.py:78
  1018.5 0.0 copy-done.1
  (13 shorter events, 0.1 us)
Async XLA Ops:
  8.0 15.1 %copy-start = (bf16[384,3,96]{0,2,1:T(8,128)(2,1)S(1)}, bf16[384,3,96]{0,2,1:T(8,128)(2,1)}, u32[]{:S(2)}) copy-start(bf16[384,3,96]{0,2,1:T(8,128)(2,1)} %param.9) | copy-start | bytes 663556
  8.1 946.5 %all-reduce.8.cloned.1.call-start = ((), (), s32[]{:S(2)}) async-start(), calls=%async_computation.2 | async-start | bytes 100663296 | tf_op jit(solution)/shard_map/psum | solution.py:65
  8.1 8.4 copy-start.2
  16.4 6.7 copy-start.5
  16.4 6.7 copy-start.9
  30.9 3.7 copy-start.3
  74.1 11.8 %copy-start.6 = (f32[2,48]{1,0:T(2,128)S(1)}, f32[2,48]{1,0:T(2,128)}, u32[]{:S(2)}) copy-start(f32[2,48]{1,0:T(2,128)} %get-tuple-element.19) | copy-start | bytes 1156
  74.1 11.8 %copy-start.7 = (f32[2,48]{1,0:T(2,128)S(1)}, f32[2,48]{1,0:T(2,128)}, u32[]{:S(2)}) copy-start(f32[2,48]{1,0:T(2,128)} %get-tuple-element.20) | copy-start | bytes 1156
  97.6 11.1 %copy-start.4 = (bf16[2,16384,48]{1,2,0:T(8,128)(2,1)S(1)}, bf16[2,16384,48]{1,2,0:T(8,128)(2,1)}, u32[]{:S(2)}) copy-start(bf16[2,16384,48]{1,2,0:T(8,128)(2,1)} %convolution_convert_fusion.1) | copy-start | bytes 9437188
  97.6 11.1 %copy-start.11 = (bf16[16384,2,48]{0,2,1:T(8,128)(2,1)S(1)}, bf16[16384,2,48]{0,2,1:T(8,128)(2,1)}, u32[]{:S(2)}) copy-start(bf16[16384,2,48]{0,2,1:T(8,128)(2,1)} %fusion.21) | copy-start | bytes 9437188
  97.6 11.1 %copy-start.12 = (bf16[16384,2,48]{0,2,1:T(8,128)(2,1)S(1)}, bf16[16384,2,48]{0,2,1:T(8,128)(2,1)}, u32[]{:S(2)}) copy-start(bf16[16384,2,48]{0,2,1:T(8,128)(2,1)} %fusion.22) | copy-start | bytes 9437188
  121.0 27.3 %copy-start.10 = (f32[384]{0:T(512)S(1)}, f32[384]{0:T(512)}, u32[]{:S(2)}) copy-start(f32[384]{0:T(512)} %param.12) | copy-start | bytes 4612
  121.0 897.5 %reduce-scatter.4.cloned.1.call-start = ((), (), s32[]{:S(2)}) async-start(), calls=%async_computation.1 | async-start | bytes 663552 | tf_op jit(solution)/shard_map/reduce_scatter | solution.py:76
  145.0 34.4 %collective-permute-start = (f32[16,384]{1,0:T(8,128)S(1)}, f32[16,384]{1,0:T(8,128)S(1)}, u32[]{:S(2)}, u32[]{:S(2)}) collective-permute-start(f32[16,384]{1,0:T(8,128)S(1)} %fusion), channel_id=1, source_target_pairs={{0,1},{1,2},{2,3},{3,4},{4,5},{5,6},{6,7},{8,9},{9,10},{10,11},{11... | collective-permute-start | bytes 73736
  146.9 17.8 %copy-start.13 = (u32[32]{0:T(128)S(1)}, u32[32]{0:T(128)}, u32[]{:S(2)}) copy-start(u32[32]{0:T(128)} %constant.26) | copy-start | bytes 388
  147.0 31.2 %copy-start.8 = (u32[32]{0:T(128)S(1)}, u32[32]{0:T(128)}, u32[]{:S(2)}) copy-start(u32[32]{0:T(128)} %constant.34) | copy-start | bytes 388
  147.0 32.4 %collective-permute-start.1 = (f32[12,384]{1,0:T(8,128)S(1)}, f32[12,384]{1,0:T(8,128)S(1)}, u32[]{:S(2)}, u32[]{:S(2)}) collective-permute-start(f32[12,384]{1,0:T(8,128)S(1)} %slice.15), channel_id=1, source_target_pairs={{0,2},{1,3},{2,4},{3,5},{4,6},{5,7},{8,10},{9,11},{10,12},{11,13},... | collective-permute-start | bytes 55304
  972.4 46.1 %copy-start.1 = (bf16[384,3,96]{0,2,1:T(8,128)(2,1)S(1)}, bf16[384,3,96]{0,2,1:T(8,128)(2,1)}, u32[]{:S(2)}) copy-start(bf16[384,3,96]{0,2,1:T(8,128)(2,1)} %param.9) | copy-start | bytes 663556
Sparse Core Ops, SparseCore 0:
  121.1 833.4 all-reduce.7
Sparse Core Ops, SparseCore 1:
  166.3 29.3 reduce-scatter.3
where the time goes:
time: 1030 us
  waiting for transfers between devices  774 us (75%)
  matrix products  84.6 us (8%)
  other arithmetic  71.9 us (7%)
  blocking collectives  68.8 us (7%)
  between operations  17.1 us (2%)
    psum x1, waiting for transfers between devices, local_step(): lax.psum(y_part, 'tp')  774 us
    convert_element_type x1, other arithmetic, local_step(): (grad_blk.astype(jnp.float32) + layer_norm_bwd(grad_u, x_hat, inv_std, ln...  32.7 us
    unnamed x2, blocking collectives  29 us
    psum x1, blocking collectives, local_step(): gram_mat, q_sq, k_sq = lax.psum((gram_part, q_part, k_part), 'sp')  26.5 us
  transfers between devices with their start and end apart: 4, of which 1 were waited for; matrix products, arithmetic and copies ran while one was open for 9% of the time, Pallas kernels for 0%

commit v1 on v0

v1 whole, which is shorter than its diff:
```python
import functools

import jax
import jax.numpy as jnp
from jax import lax
from jax.experimental import pallas as pl
from jax.experimental.pallas import tpu as pltpu
from jax.sharding import PartitionSpec as P

F32, BF16 = jnp.float32, jnp.bfloat16
LN_EPS = 1e-6
NT = 256
CH = 64
MESH = pl.DeviceIdType.MESH


def dot(a, b):
    return jnp.dot(a, b, preferred_element_type=F32)


def dot_nt(a, b):
    return lax.dot_general(a, b, (((1,), (1,)), ((), ())), preferred_element_type=F32)


def fold8(v):
    return jnp.sum(v.reshape(v.shape[0] // 8, 8, v.shape[1]), axis=0)


def ln_stats(xt, cols):
    d = xt.shape[0]
    acc = jnp.zeros((8, NT), F32)
    for c in range(0, d, CH):
        acc = acc + fold8(xt[c : c + CH, cols].astype(F32))
    mean = jnp.sum(acc, axis=0, keepdims=True) * (1.0 / d)
    acc = jnp.zeros((8, NT), F32)
    for c in range(0, d, CH):
        v = xt[c : c + CH, cols].astype(F32) - mean
        acc = acc + fold8(v * v)
    inv = lax.rsqrt(jnp.sum(acc, axis=0, keepdims=True) * (1.0 / d) + LN_EPS)
    return mean, inv


def spread_columns(row_ref, out):
    d = row_ref.shape[1]
    out[...] = jnp.broadcast_to(row_ref[...], (NT, d)).T


def stats_kernel(steps, x_ref, g_ref, w_ref, gam_ref, bet_ref, out_ref, wq, gam, bet, xt, ut, qd, kv, acc, sq):
    step = pl.program_id(0)
    rows, d = x_ref.shape
    own = w_ref.shape[1]
    head = out_ref.shape[0] // 2

    @pl.when(step == 0)
    def _():
        for e in range(3):
            wq[e * own : (e + 1) * own, :] = w_ref[e]
        spread_columns(gam_ref, gam)
        spread_columns(bet_ref, bet)
        acc[...] = jnp.zeros_like(acc)
        sq[...] = jnp.zeros_like(sq)

    for n in range(rows // NT):
        cols = pl.ds(n * NT, NT)
        xt[:, cols] = x_ref[pl.ds(n * NT, NT), :].T
        mean, inv = ln_stats(xt, cols)
        for c in range(0, d, CH):
            v = (xt[c : c + CH, cols].astype(F32) - mean) * inv
            ut[c : c + CH, cols] = (v * gam[c : c + CH, :] + bet[c : c + CH, :]).astype(BF16)
    for n in range(rows // NT):
        cols = pl.ds(n * NT, NT)
        qkv = dot(wq[...], ut[:, cols]).astype(BF16)
        qd[0:own, cols] = qkv[0:own]
        kv[:, cols] = qkv[own:]
        qd[own:, cols] = dot_nt(w_ref[3], g_ref[pl.ds(n * NT, NT), :]).astype(BF16)
    for n in range(rows // NT):
        cols = pl.ds(n * NT, NT)
        for e, ref in enumerate((qd, kv)):
            v = ref[0:own, cols].astype(F32)
            v = v * v
            sq[e] += v[:, :128] + v[:, 128:]
    acc[:, 0 : 2 * own] += dot_nt(qd[...], kv[...])

    @pl.when(step == steps - 1)
    def _():
        lane = lax.broadcasted_iota(jnp.int32, (head, 128), 1)
        for h in range(own // head):
            r = h * head
            gram = pltpu.roll(acc[r : r + head, :], 256 - r, 1)[:, :128] if r else acc[r : r + head, :][:, :128]
            datt = pltpu.roll(acc[own + r : own + r + head, :], 256 - (own + r) + head, 1)[:, :128]
            q2 = jnp.sum(sq[0, r : r + head, :], axis=1, keepdims=True)
            k2 = jnp.sum(sq[1, r : r + head, :], axis=1, keepdims=True)
            v = jnp.where(lane < head, gram, datt)
            v = jnp.where(lane == 2 * head, q2, v)
            out_ref[r : r + head, :] = jnp.where(lane == 2 * head + 1, k2, v)


def stats_call(x, g, w, gam, bet, heads_loc, block=1024):
    rows, d = x.shape
    own = w.shape[1]
    steps = rows // block
    row = pl.BlockSpec((block, d), lambda i: (i, 0))
    full = lambda a: pl.BlockSpec(a.shape, lambda i: (0,) * a.ndim)
    return pl.pallas_call(
        functools.partial(stats_kernel, steps),
        grid=(steps,),
        in_specs=[row, row, full(w), full(gam), full(bet)],
        out_specs=pl.BlockSpec((own, 128), lambda i: (0, 0)),
        out_shape=jax.ShapeDtypeStruct((own, 128), F32),
        scratch_shapes=[
            pltpu.VMEM((3 * own, d), BF16),
            pltpu.VMEM((d, NT), F32),
            pltpu.VMEM((d, NT), F32),
            pltpu.VMEM((d, block), BF16),
            pltpu.VMEM((d, block), BF16),
            pltpu.VMEM((2 * own, block), BF16),
            pltpu.VMEM((2 * own, block), BF16),
            pltpu.VMEM((2 * own, 256), F32),
            pltpu.VMEM((2, own, 128), F32),
        ],
        compiler_params=pltpu.CompilerParams(dimension_semantics=("arbitrary",), vmem_limit_bytes=40 * 2**20),
        cost_estimate=pl.CostEstimate(flops=2 * rows * d * 4 * own, bytes_accessed=4 * rows * d, transcendentals=0),
        name="stats",
    )(x, g, w, gam, bet)


def greet(barrier, peers):
    for peer in peers:
        pl.semaphore_signal(barrier, inc=1, device_id=peer, device_id_type=MESH)
    pl.semaphore_wait(barrier, len(peers))


def state_kernel(tp, sp, s_ref, temp_ref, m1_ref, m2_ref, cq_ref, ck_ref, dt_ref, parts, state, big, send_a, recv_a, send_b, recv_b):
    my_sp, my_tp = lax.axis_index("sp"), lax.axis_index("tp")
    own = s_ref.shape[0]
    heads_loc = temp_ref.shape[0] // tp
    head = own // heads_loc
    d = own * tp
    sp_peers = [{"sp": lax.rem(my_sp + k, sp)} for k in range(1, sp)]
    tp_peers = [{"tp": lax.rem(my_tp + k, tp)} for k in range(1, tp)]
    greet(pltpu.get_barrier_semaphore(), sp_peers + tp_peers)

    copies = []
    for k in range(1, sp):
        copies.append(
            pltpu.make_async_remote_copy(
                src_ref=s_ref,
                dst_ref=parts.at[my_sp],
                send_sem=send_a.at[k],
                recv_sem=recv_a.at[k],
                device_id=sp_peers[k - 1],
                device_id_type=MESH,
            )
        )
        copies[-1].start()
    parts[my_sp] = s_ref[...]
    big[...] = jnp.zeros_like(big)
    for c in copies:
        c.wait()
    total = parts[0]
    for k in range(1, sp):
        total = total + parts[k]

    lane = lax.broadcasted_iota(jnp.int32, (head, 128), 1)
    row = lax.broadcasted_iota(jnp.int32, (head, 128), 0)
    valid = lane < head
    eye = lane == row
    pick = lambda t, i: jnp.sum(jnp.where(lane == i, t, 0.0), axis=1, keepdims=True)
    for h in range(heads_loc):
        t = total[h * head : (h + 1) * head, :]
        tau = temp_ref[my_tp * heads_loc + h]
        gram = t
        datt = pltpu.roll(t, 128 - head, 1)
        q2 = pick(t, 2 * head)
        k2c = pick(t, 2 * head + 1)
        k2 = jnp.sum(jnp.where(eye, k2c, 0.0), axis=0, keepdims=True)
        k2 = jnp.where(valid, k2, 1.0)
        norm = jnp.sqrt(q2) * jnp.sqrt(k2)
        gram_n = jnp.where(valid, gram / norm, 0.0)
        datt = jnp.where(valid, datt, 0.0)
        logit = jnp.where(valid, tau * gram_n, -1e30)
        ex = jnp.exp(logit - jnp.max(logit, axis=1, keepdims=True))
        ex = jnp.where(valid, ex, 0.0)
        att = ex / jnp.sum(ex, axis=1, keepdims=True)
        d_logit = att * (datt - jnp.sum(att * datt, axis=1, keepdims=True))
        d_tau = jnp.sum(jnp.sum(d_logit * gram_n, axis=1, keepdims=True), axis=0, keepdims=True)
        e_mat = tau * d_logit
        d_gram = (e_mat / norm).astype(BF16).astype(F32)
        es = e_mat * gram_n
        q_coef = -jnp.sum(es, axis=1, keepdims=True) / q2
        k_coef = -jnp.sum(es, axis=0, keepdims=True) / k2
        k_coef = jnp.sum(jnp.where(eye, k_coef, 0.0), axis=1, keepdims=True)
        v = jnp.where(valid, att.astype(BF16).astype(F32), pltpu.roll(d_gram, head, 1))
        v = jnp.where(lane == 2 * head, q_coef, v)
        v = jnp.where(lane == 2 * head + 1, k_coef, v)
        v = jnp.where(lane == 2 * head + 2, d_tau, v)
        state[0, h * head : (h + 1) * head, :] = v

    copies = []
    for k in range(1, tp):
        copies.append(
            pltpu.make_async_remote_copy(
                src_ref=state.at[0],
                dst_ref=state.at[tp - k],
                send_sem=send_b.at[k],
                recv_sem=recv_b.at[k],
                device_id=tp_peers[k - 1],
                device_id_type=MESH,
            )
        )
        copies[-1].start()
    for c in copies:
        c.wait()

    head_row = lax.broadcasted_iota(jnp.int32, dt_ref.shape, 0)
    dt = jnp.zeros(dt_ref.shape, F32)
    zero = jnp.zeros((head, d - 128), F32)
    for j in range(tp):
        for h in range(heads_loc):
            t = state[j, h * head : (h + 1) * head, :]
            r = j * own + h * head
            att = jnp.concatenate([jnp.where(valid, t, 0.0), zero], axis=1)
            d_gram = jnp.concatenate([jnp.where(valid, pltpu.roll(t, 128 - head, 1), 0.0), zero], axis=1)
            big[0, r : r + head, :] = pltpu.roll(att, r, 1) if r else att
            big[1, r : r + head, :] = pltpu.roll(d_gram, r, 1) if r else d_gram
            cq_ref[r : r + head, :] = jnp.broadcast_to(pick(t, 2 * head), (head, NT))
            ck_ref[r : r + head, :] = jnp.broadcast_to(pick(t, 2 * head + 1), (head, NT))
            which = lax.rem(my_tp + j, tp) * heads_loc + h
            dt = jnp.where(head_row == which, pick(t, 2 * head + 2)[0:1, :], dt)
    dt_ref[...] = dt
    low = m1_ref.shape[1]
    for i in range(2):
        m = big[i].astype(BF16)
        mt = m.T
        m1_ref[2 * i] = m[0:low, 0:256]
        m2_ref[2 * i] = m[low:, 128:]
        m1_ref[2 * i + 1] = mt[0:low, 0:256]
        m2_ref[2 * i + 1] = mt[low:, 128:]


def state_call(s, temps, tp, sp):
    own = s.shape[0]
    d = own * tp
    head = d // temps.shape[0]
    low = 256 // head * head
    vmem = pl.BlockSpec(memory_space=pltpu.VMEM)
    return pl.pallas_call(
        functools.partial(state_kernel, tp, sp),
        in_specs=[vmem, pl.BlockSpec(memory_space=pltpu.SMEM)],
        out_specs=[vmem] * 5,
        out_shape=[
            jax.ShapeDtypeStruct((4, low, 256), BF16),
            jax.ShapeDtypeStruct((4, d - low, 256), BF16),
            jax.ShapeDtypeStruct((d, NT), F32),
            jax.ShapeDtypeStruct((d, NT), F32),
            jax.ShapeDtypeStruct((temps.shape[0], 128), F32),
        ],
        scratch_shapes=[
            pltpu.VMEM((sp, own, 128), F32),
            pltpu.VMEM((tp, own, 128), F32),
            pltpu.VMEM((2, d, d), F32),
            pltpu.SemaphoreType.DMA((sp,)),
            pltpu.SemaphoreType.DMA((sp,)),
            pltpu.SemaphoreType.DMA((tp,)),
            pltpu.SemaphoreType.DMA((tp,)),
        ],
        compiler_params=pltpu.CompilerParams(collective_id=0, has_side_effects=True),
        name="state",
    )(s, temps)


def main_kernel(steps, x_ref, g_ref, w0, w1, w2, w3, m1, m2, gam_ref, bet_ref, cq, ck, y_ref, dx_ref, dw_ref,
                wt, wn, wo, wot, gam, bet, xt, ut, xh, qkv, do, ot, rt, gx, inv_s, acc_w, acc_o, acc_g):
    step = pl.program_id(0)
    rows, d = x_ref.shape
    pieces = (w0, w1, w2, w3)
    own = w0.shape[1]
    low = m1.shape[1]

    @pl.when(step == 0)
    def _():
        for j, piece in enumerate(pieces):
            for e in range(3):
                wt[e * d + j * own : e * d + (j + 1) * own, :] = piece[e]
            wo[j * own : (j + 1) * own, :] = piece[3]
        for e in range(3):
            wn[:, e * d : (e + 1) * d] = wt[e * d : (e + 1) * d, :].T
        wot[...] = wo[...].T
        spread_columns(gam_ref, gam)
        spread_columns(bet_ref, bet)
        acc_w[...] = jnp.zeros_like(acc_w)
        acc_o[...] = jnp.zeros_like(acc_o)
        acc_g[...] = jnp.zeros_like(acc_g)

    tiles = [(pl.ds(n * NT, NT), pl.ds(n * NT, NT)) for n in range(rows // NT)]
    for cols, _ in tiles:
        xt[:, cols] = x_ref[cols, :].T
        mean, inv = ln_stats(xt, cols)
        inv_s[:, cols] = jnp.broadcast_to(inv, (8, NT))
        for c in range(0, d, CH):
            v = (xt[c : c + CH, cols].astype(F32) - mean) * inv
            xh[c : c + CH, cols] = v
            ut[c : c + CH, cols] = (v * gam[c : c + CH, :] + bet[c : c + CH, :]).astype(BF16)
    for cols, _ in tiles:
        qkv[:, cols] = dot(wt[...], ut[:, cols]).astype(BF16)
        do[:, cols] = dot_nt(wo[...], g_ref[cols, :]).astype(BF16)
    for cols, _ in tiles:
        ot[0:low, cols] = dot(m1[0], qkv[2 * d : 2 * d + 256, cols]).astype(BF16)
        ot[low:d, cols] = dot(m2[0], qkv[2 * d + 128 : 3 * d, cols]).astype(BF16)
        rt[2 * d : 2 * d + low, cols] = dot(m1[1], do[0:256, cols]).astype(BF16)
        rt[2 * d + low : 3 * d, cols] = dot(m2[1], do[128:d, cols]).astype(BF16)
        for part, other, coef, i in ((0, d, cq, 2), (d, 0, ck, 3)):
            v = dot(m1[i], qkv[other : other + 256, cols])
            rt[part : part + low, cols] = (v + qkv[part : part + low, cols].astype(F32) * coef[0:low, :]).astype(BF16)
            v = dot(m2[i], qkv[other + 128 : other + d, cols])
            rt[part + low : part + d, cols] = (v + qkv[part + low : part + d, cols].astype(F32) * coef[low:d, :]).astype(BF16)
    for cols, _ in tiles:
        yt = dot(wot[...], ot[:, cols]) + xt[:, cols].astype(F32)
        y_ref[cols, :] = yt.astype(BF16).T
        gx[:, cols] = dot(wn[...], rt[:, cols])
    for cols, _ in tiles:
        s1 = jnp.zeros((8, NT), F32)
        s2 = jnp.zeros((8, NT), F32)
        for c in range(0, d, CH):
            du = gx[c : c + CH, cols]
            h = xh[c : c + CH, cols]
            acc_g[0, c : c + CH, :] += du * h
            acc_g[1, c : c + CH, :] += du
            a = du * gam[c : c + CH, :]
            s1 = s1 + fold8(a)
            s2 = s2 + fold8(a * h)
            gx[c : c + CH, cols] = a
        mean1 = jnp.sum(s1, axis=0, keepdims=True) * (1.0 / d)
        mean2 = jnp.sum(s2, axis=0, keepdims=True) * (1.0 / d)
        inv = inv_s[0:1, cols]
        for c in range(0, d, CH):
            gx[c : c + CH, cols] = inv * (gx[c : c + CH, cols] - mean1 - xh[c : c + CH, cols] * mean2)
        dxt = gx[:, cols] + g_ref[cols, :].T.astype(F32)
        dx_ref[cols, :] = dxt.astype(BF16).T
    r_own = jnp.concatenate([rt[e * d : e * d + own, :] for e in range(3)], axis=0)
    acc_w[...] += dot_nt(r_own, ut[...])
    acc_o[...] += dot(ot[0:own, :], g_ref[...])

    @pl.when(step == steps - 1)
    def _():
        sp, slot_rows = dw_ref.shape[0], dw_ref.shape[1]
        per = d // sp
        sub = own // sp
        wgrad = acc_w[...].T
        for s in range(sp):
            dw_ref[s, 0:per, 0 : 3 * own] = wgrad[s * per : (s + 1) * per, :]
            for q in range(d // own):
                dw_ref[s, q * sub : (q + 1) * sub, 3 * own :] = acc_o[s * sub : (s + 1) * sub, q * own : (q + 1) * own]
        zero = jnp.zeros((slot_rows - per - 2, d), F32)
        gb = jnp.concatenate([jnp.sum(acc_g[i].T, axis=0, keepdims=True) for i in range(2)] + [zero], axis=0)
        for s in range(sp):
            dw_ref[s, per:slot_rows, :] = gb


def main_call(x, g, pieces, m1, m2, gam, bet, cq, ck, sp, block=1024):
    rows, d = x.shape
    own = pieces[0].shape[1]
    steps = rows // block
    row = pl.BlockSpec((block, d), lambda i: (i, 0))
    full = lambda a: pl.BlockSpec(a.shape, lambda i: (0,) * a.ndim)
    slot = (sp, d // sp + 8, d)
    smalls = (*pieces, m1, m2, gam, bet, cq, ck)
    return pl.pallas_call(
        functools.partial(main_kernel, steps),
        grid=(steps,),
        in_specs=[row, row] + [full(a) for a in smalls],
        out_specs=[row, row, pl.BlockSpec(slot, lambda i: (0, 0, 0))],
        out_shape=[jax.ShapeDtypeStruct((rows, d), BF16), jax.ShapeDtypeStruct((rows, d), BF16), jax.ShapeDtypeStruct(slot, F32)],
        scratch_shapes=[
            pltpu.VMEM((3 * d, d), BF16),
            pltpu.VMEM((d, 3 * d), BF16),
            pltpu.VMEM((d, d), BF16),
            pltpu.VMEM((d, d), BF16),
            pltpu.VMEM((d, NT), F32),
            pltpu.VMEM((d, NT), F32),
            pltpu.VMEM((d, block), BF16),
            pltpu.VMEM((d, block), BF16),
            pltpu.VMEM((d, block), F32),
            pltpu.VMEM((3 * d, block), BF16),
            pltpu.VMEM((d, block), BF16),
            pltpu.VMEM((d, block), BF16),
            pltpu.VMEM((3 * d, block), BF16),
            pltpu.VMEM((d, block), F32),
            pltpu.VMEM((8, block), F32),
            pltpu.VMEM((3 * own, d), F32),
            pltpu.VMEM((own, d), F32),
            pltpu.VMEM((2, d, NT), F32),
        ],
        compiler_params=pltpu.CompilerParams(dimension_semantics=("arbitrary",), vmem_limit_bytes=60 * 2**20),
        cost_estimate=pl.CostEstimate(flops=2 * rows * d * d * 9, bytes_accessed=8 * rows * d, transcendentals=0),
        name="main",
    )(x, g, *smalls)


def wgrad_kernel(sp, in_ref, out_ref, pair, got, send_a, recv_a, send_b, recv_b):
    my = lax.axis_index("sp")
    chips = sp // 2
    core, chip = lax.rem(my, 2), my // 2
    other = {"sp": chip * 2 + 1 - core}
    peers = [{"sp": lax.rem(chip + k, chips) * 2 + core} for k in range(1, chips)]
    greet(pltpu.get_barrier_semaphore(), [other] + peers)
    first = []
    for c in range(chips):
        first.append(
            pltpu.make_async_remote_copy(
                src_ref=in_ref.at[2 * c + 1 - core],
                dst_ref=pair.at[c],
                send_sem=send_a.at[c],
                recv_sem=recv_a.at[c],
                device_id=other,
                device_id_type=MESH,
            )
        )
        first[-1].start()
    for c in range(chips):
        first[c].wait()
    for c in range(chips):
        got[chips + c] = in_ref[2 * c + core] + pair[c]
    second = []
    for k in range(1, chips):
        second.append(
            pltpu.make_async_remote_copy(
                src_ref=got.at[chips + lax.rem(chip + k, chips)],
                dst_ref=got.at[chip],
                send_sem=send_b.at[k],
                recv_sem=recv_b.at[k],
                device_id=peers[k - 1],
                device_id_type=MESH,
            )
        )
        second[-1].start()
    got[chip] = got[chips + chip]
    for c in second:
        c.wait()
    total = got[0]
    for c in range(1, chips):
        total = total + got[c]
    out_ref[...] = total


def wgrad_call(parts):
    sp, slot = parts.shape[0], parts.shape[1:]
    vmem = pl.BlockSpec(memory_space=pltpu.VMEM)
    return pl.pallas_call(
        functools.partial(wgrad_kernel, sp),
        in_specs=[vmem],
        out_specs=vmem,
        out_shape=jax.ShapeDtypeStruct(slot, F32),
        scratch_shapes=[
            pltpu.VMEM((sp // 2, *slot), F32),
            pltpu.VMEM((sp, *slot), F32),
            pltpu.SemaphoreType.DMA((sp // 2,)),
            pltpu.SemaphoreType.DMA((sp // 2,)),
            pltpu.SemaphoreType.DMA((sp // 2,)),
            pltpu.SemaphoreType.DMA((sp // 2,)),
        ],
        compiler_params=pltpu.CompilerParams(collective_id=1, has_side_effects=True),
        name="wgrad",
    )(parts)


def solution(mesh):
    tp, sp = mesh.shape["tp"], mesh.shape["sp"]
    row_spec = P(("dp", "sp"), None)

    def local_step(x, g, w_qkv, w_out, gamma, beta, temps):
        d = x.shape[1]
        own = w_qkv.shape[2]
        heads_loc = temps.shape[0] // tp
        gam, bet = gamma.reshape(1, d), beta.reshape(1, d)
        piece = jnp.concatenate([w_qkv.transpose(1, 2, 0), w_out[None]], axis=0)
        pieces = [piece]
        for j in range(1, tp):
            pieces.append(lax.ppermute(piece, "tp", [(i, (i - j) % tp) for i in range(tp)]))
        s = stats_call(x, g, piece, gam, bet, heads_loc)
        m1, m2, cq, ck, dt = state_call(s, temps, tp, sp)
        y, dx, parts = main_call(x, g, pieces, m1, m2, gam, bet, cq, ck, sp)
        got = wgrad_call(parts)
        per = d // sp
        sub = own // sp
        grad_wqkv = got[:per, : 3 * own].reshape(per, 3, own)
        grad_wout = got[:per, 3 * own :].reshape(tp, sub, own).transpose(1, 0, 2).reshape(sub, d)
        return y, dx, grad_wqkv, grad_wout, got[per], got[per + 1], dt[:, 0]

    in_specs = (row_spec, row_spec, P(None, None, "tp"), P("tp", None), P(None), P(None), P(None))
    out_specs = (row_spec, row_spec, P(("dp", "sp"), None, "tp"), P(("dp", "tp", "sp"), None), P("dp"), P("dp"), P("dp"))
    return jax.shard_map(local_step, mesh=mesh, in_specs=in_specs, out_specs=out_specs, check_vma=False)
```

time: 1030 us -> 166 us (0.16)
  waiting for transfers between devices: 774 us -> 0.01 us
  Pallas kernels: 0 us -> 143 us
  matrix products: 84.6 us -> 0 us
  other arithmetic: 71.9 us -> 1.01 us
  blocking collectives: 68.8 us -> 0 us
  between operations: 17.1 us -> 0.75 us
    psum x1 -> x0, waiting for transfers between devices: 774 us -> none  [local_step(): lax.psum(y_part, 'tp')]
    pallas_call x0 -> x4, Pallas kernels: none -> 143 us  [the longest x1 88.7 us: main_call(): pl.pallas_call(functools.partial(main_kernel, steps), grid=(steps,), in_s...]
    dot_general x11 -> x0, matrix products: 77.9 us -> none  [the longest x1 16.4 us: local_step(): jnp.einsum('nd,nec->dec', u_act, dqkv_act, preferred_element_type=jnp.flo...]
    psum x2 -> x0, blocking collectives: 39.8 us -> none  [the longest x1 26.5 us: local_step(): gram_mat, q_sq, k_sq = lax.psum((gram_part, q_part, k_part), 'sp')]
    convert_element_type x2 -> x0, other arithmetic: 33.7 us -> none  [the longest x1 32.7 us: local_step(): (grad_blk.astype(jnp.float32) + layer_norm_bwd(grad_u, x_hat, inv_std, ln...]
    reduce_sum x3 -> x0, other arithmetic: 32.6 us -> none  [the longest x1 17.8 us: local_step(): jnp.sum(grad_u * x_hat, axis=0)]
    unnamed x2 -> x0, blocking collectives: 29 us -> none
  transfers between devices with their start and end apart: 4 -> 3, of which waited for: 1 -> 0; matrix products, arithmetic and copies ran while one was open for 9% -> 2% of each run, Pallas kernels for 0% -> 26%
where the time goes in v1:
time: 166 us; the launch traced here: 165 us
  Pallas kernels  143 us (86%)
  local copies, waits for them, and re-layouts  13.3 us (8%)
  starting transfers between devices  6.99 us (4%)
    pallas_call x1, Pallas kernels, main_call(): pl.pallas_call(functools.partial(main_kernel, steps), grid=(steps,), in_s...  88.7 us
    pallas_call x1, Pallas kernels, stats_call(): pl.pallas_call(functools.partial(stats_kernel, steps), grid=(steps,), in_...  24.1 us
    pallas_call x1, Pallas kernels, state_call(): pl.pallas_call(functools.partial(state_kernel, tp, sp), in_specs=[vmem, p...  18.7 us
    pallas_call x1, Pallas kernels, wgrad_call(): pl.pallas_call(functools.partial(wgrad_kernel, sp), in_specs=[vmem], out_...  11.6 us
    ppermute x3, starting transfers between devices, local_step(): lax.ppermute(piece, 'tp', [(i, (i - j) % tp) for i in range(tp)])  6.99 us
    unnamed x17, local copies, waits for them, and re-layouts  6.75 us
  transfers between devices with their start and end apart: 3, of which 0 were waited for; matrix products, arithmetic and copies ran while one was open for 2% of the time, Pallas kernels for 26%

profile of v1, /device:TPU:97, one launch (start us, length us, event | category | flops | bytes accessed | tf_op | source)
XLA Modules:
  0.0 165.1 jit_solution(12621868253315272297)
XLA Ops:
  0.6 1.0 pad_maximum_fusion.w_ref.w0
  1.6 0.0 copy-start.1
  1.7 2.8 %collective-permute-start.2 = (bf16[4,96,384]{2,1,0:T(8,128)(2,1)S(1)}, bf16[4,96,384]{2,1,0:T(8,128)(2,1)S(1)}, u32[]{:S(2)}, u32[]{:S(2)}) collective-permute-start(bf16[4,96,384]{2,1,0:T(8,128)(2,1)S(1)} %pad_maximum_fusion.w_ref.w0), channel_id=1, source_target_pairs={{0,8},{8,16},{16,24},{24,0},{1,9},{9,17},{17,25},{25,1},{2,10},{10... | collective-permute-start | bytes 884744 | tf_op jit(solution)/shard_map/ppermute | solution.py:479
  4.4 3.7 %collective-permute-start.1 = (bf16[4,96,384]{2,1,0:T(8,128)(2,1)S(1)}, bf16[4,96,384]{2,1,0:T(8,128)(2,1)S(1)}, u32[]{:S(2)}, u32[]{:S(2)}) collective-permute-start(bf16[4,96,384]{2,1,0:T(8,128)(2,1)S(1)} %pad_maximum_fusion.w_ref.w0), channel_id=1, source_target_pairs={{0,16},{8,24},{16,0},{24,8},{1,17},{9,25},{17,1},{25,9},{2,18},{10... | collective-permute-start | bytes 884744 | tf_op jit(solution)/shard_map/ppermute | solution.py:479
  8.1 0.5 collective-permute-start
  8.6 0.7 reshape.29.gam_ref
  9.3 0.0 copy-start.3
  9.3 0.7 reshape.30.bet_ref
  10.0 0.0 copy-start
  10.0 4.6 %copy-done = bf16[16384,384]{1,0:T(8,128)(2,1)S(1)} copy-done((bf16[16384,384]{1,0:T(8,128)(2,1)S(1)}, bf16[16384,384]{1,0:T(8,128)(2,1)}, u32[]{:S(2)}) %copy-start) | copy-done | bytes 12582936
  14.6 0.0 copy-start.4
  14.6 24.1 %stats.1.s_ref = f32[96,128]{1,0:T(8,128)S(1)} custom-call(bf16[16384,384]{1,0:T(8,128)(2,1)S(1)} %copy-done, bf16[16384,384]{1,0:T(8,128)(2,1)} %g_ref.3, bf16[4,96,384]{2,1,0:T(8,128)(2,1)S(1)} %pad_maximum_fusion.w_ref.w0, f32[1,384]{1,0:T(1,128)S(1)} %reshape.29.gam_ref, f32[1,384]{1,0:T(1,128)S(1)} %reshape.30.bet_ref), custom_call_target="tpu_custom_call" | custom-call | flops 4831838208 | bytes 25165824 | tf_op jit(solution)/shard_map/stats/pallas_call | solution.py:104
  38.7 0.0 copy-done.1
  38.7 0.0 copy-done.3
  38.7 0.0 copy-done.4
  38.7 0.0 copy-start.2
  38.7 0.6 copy-done.2
  39.4 18.7 %state.1 = (bf16[4,240,256]{2,1,0:T(8,128)(2,1)}, bf16[4,144,256]{2,1,0:T(8,128)(2,1)}, f32[384,256]{1,0:T(8,128)}, f32[384,256]{1,0:T(8,128)}, f32[8,128]{1,0:T(8,128)}) custom-call(f32[96,128]{1,0:T(8,128)} %copy-done.2, f32[8]{0:T(128)} %temp_ref.1), custom_call_target="tpu_custom_call" | custom-call | tf_op jit(solution)/shard_map/state/pallas_call | solution.py:247
  58.1 1.3 slice_reduce_fusion
  59.4 0.0 collective-permute-done.2.w3
  59.4 0.0 copy-start.5
  59.4 0.0 collective-permute-done.1.w2
  59.4 0.0 copy-start.6
  59.4 0.0 collective-permute-done.w1
  59.4 0.0 copy-start.7
  59.4 0.7 copy-done.5
  60.1 0.1 copy-done.6
  60.2 0.1 copy-done.7
  60.3 88.7 %main.1 = (bf16[16384,384]{1,0:T(8,128)(2,1)}, bf16[16384,384]{1,0:T(8,128)(2,1)}, f32[8,56,384]{2,1,0:T(8,128)}) custom-call(bf16[16384,384]{1,0:T(8,128)(2,1)} %x_ref.3, bf16[16384,384]{1,0:T(8,128)(2,1)} %g_ref.3, bf16[4,96,384]{2,1,0:T(8,128)(2,1)} %copy-done.1, bf16[4,96,384]{2,1,0:T(8,128)(2,1)} %copy-done.7, bf16[4,96,384]{2,1,0:T(8,128)(2,1)} %copy-done.6, ...), custom_call_target="tpu_custom_call" | custom-call | flops 43486543872 | bytes 50331648 | tf_op jit(solution)/shard_map/main/pallas_call | solution.py:368
  149.0 11.6 %wgrad.1 = f32[56,384]{1,0:T(8,128)} custom-call(f32[8,56,384]{2,1,0:T(8,128)} %get-tuple-element.21.in_ref), custom_call_target="tpu_custom_call" | custom-call | tf_op jit(solution)/shard_map/wgrad/pallas_call | solution.py:449
  160.6 1.4 slice_reduce_fusion.1
  161.9 0.8 slice.16
  162.8 0.9 slice.15
  163.7 0.7 reshape.33
  164.4 0.1 reshape.31
  164.5 0.6 copy.18
  (2 shorter events, 0.0 us)
Async XLA Ops:
  1.6 37.1 %copy-start.1 = (bf16[4,96,384]{2,1,0:T(8,128)(2,1)}, bf16[4,96,384]{2,1,0:T(8,128)(2,1)S(1)}, u32[]{:S(2)}) copy-start(bf16[4,96,384]{2,1,0:T(8,128)(2,1)S(1)} %pad_maximum_fusion.w_ref.w0) | copy-start | bytes 884740
  1.7 57.7 %collective-permute-start.2 = (bf16[4,96,384]{2,1,0:T(8,128)(2,1)S(1)}, bf16[4,96,384]{2,1,0:T(8,128)(2,1)S(1)}, u32[]{:S(2)}, u32[]{:S(2)}) collective-permute-start(bf16[4,96,384]{2,1,0:T(8,128)(2,1)S(1)} %pad_maximum_fusion.w_ref.w0), channel_id=1, source_target_pairs={{0,8},{8,16},{16,24},{24,0},{1,9},{9,17},{17,25},{25,1},{2,10},{10... | collective-permute-start | bytes 884744 | tf_op jit(solution)/shard_map/ppermute | solution.py:479
  4.4 55.0 %collective-permute-start.1 = (bf16[4,96,384]{2,1,0:T(8,128)(2,1)S(1)}, bf16[4,96,384]{2,1,0:T(8,128)(2,1)S(1)}, u32[]{:S(2)}, u32[]{:S(2)}) collective-permute-start(bf16[4,96,384]{2,1,0:T(8,128)(2,1)S(1)} %pad_maximum_fusion.w_ref.w0), channel_id=1, source_target_pairs={{0,16},{8,24},{16,0},{24,8},{1,17},{9,25},{17,1},{25,9},{2,18},{10... | collective-permute-start | bytes 884744 | tf_op jit(solution)/shard_map/ppermute | solution.py:479
  8.1 51.3 %collective-permute-start = (bf16[4,96,384]{2,1,0:T(8,128)(2,1)S(1)}, bf16[4,96,384]{2,1,0:T(8,128)(2,1)S(1)}, u32[]{:S(2)}, u32[]{:S(2)}) collective-permute-start(bf16[4,96,384]{2,1,0:T(8,128)(2,1)S(1)} %pad_maximum_fusion.w_ref.w0), channel_id=1, source_target_pairs={{0,24},{8,0},{16,8},{24,16},{1,25},{9,1},{17,9},{25,17},{2,26},{10... | collective-permute-start | bytes 884744 | tf_op jit(solution)/shard_map/ppermute | solution.py:479
  9.3 29.4 %copy-start.3 = (f32[1,384]{1,0:T(1,128)}, f32[1,384]{1,0:T(1,128)S(1)}, u32[]{:S(2)}) copy-start(f32[1,384]{1,0:T(1,128)S(1)} %reshape.29.gam_ref) | copy-start | bytes 4612
  10.0 4.6 %copy-start = (bf16[16384,384]{1,0:T(8,128)(2,1)S(1)}, bf16[16384,384]{1,0:T(8,128)(2,1)}, u32[]{:S(2)}) copy-start(bf16[16384,384]{1,0:T(8,128)(2,1)} %x_ref.3) | copy-start | bytes 37748740
  14.6 24.1 %copy-start.4 = (f32[1,384]{1,0:T(1,128)}, f32[1,384]{1,0:T(1,128)S(1)}, u32[]{:S(2)}) copy-start(f32[1,384]{1,0:T(1,128)S(1)} %reshape.30.bet_ref) | copy-start | bytes 4612
  38.7 0.6 copy-start.2
  59.4 0.7 copy-start.5
  59.4 0.8 copy-start.6
  59.4 0.9 copy-start.7

commit v2 on v0

v2 whole, which is shorter than its diff:
```python
import functools

import jax
import jax.numpy as jnp
from jax import lax
from jax.experimental import pallas as pl
from jax.experimental.pallas import tpu as pltpu
from jax.sharding import PartitionSpec as P

F32, BF16 = jnp.float32, jnp.bfloat16
LN_EPS = 1e-6
NT = 256
CH = 64
LANES = 128
MESH = pl.DeviceIdType.MESH


def dot(a, b):
    return jnp.dot(a, b, preferred_element_type=F32)


def dot_nt(a, b):
    return lax.dot_general(a, b, (((1,), (1,)), ((), ())), preferred_element_type=F32)


def fold8(v):
    return jnp.sum(v.reshape(v.shape[0] // 8, 8, v.shape[1]), axis=0)


def ln_stats(xt, cols):
    d = xt.shape[0]
    shift = xt[0:16, cols].astype(F32)[0:1, :]
    s1 = jnp.zeros((8, NT), F32)
    s2 = jnp.zeros((8, NT), F32)
    for c in range(0, d, CH):
        v = xt[c : c + CH, cols].astype(F32) - shift
        s1 = s1 + fold8(v)
        s2 = s2 + fold8(v * v)
    off = jnp.sum(s1, axis=0, keepdims=True) * (1.0 / d)
    var = jnp.sum(s2, axis=0, keepdims=True) * (1.0 / d) - off * off
    return shift + off, lax.rsqrt(jnp.maximum(var, 0.0) + LN_EPS)


def spread_columns(row_ref, out):
    d = row_ref.shape[0]
    out[...] = jnp.broadcast_to(row_ref[...].reshape(1, d), (NT, d)).T


def remote(src, dst, send_sem, recv_sem, device):
    return pltpu.make_async_remote_copy(
        src_ref=src, dst_ref=dst, send_sem=send_sem, recv_sem=recv_sem, device_id=device, device_id_type=MESH
    )


def head_state(t, tau, head):
    lane = lax.broadcasted_iota(jnp.int32, (head, LANES), 1)
    row = lax.broadcasted_iota(jnp.int32, (head, LANES), 0)
    valid = lane < head
    eye = lane == row
    pick = lambda i: jnp.sum(jnp.where(lane == i, t, 0.0), axis=1, keepdims=True)
    q2 = pick(2 * head)
    k2 = jnp.sum(jnp.where(eye, pick(2 * head + 1), 0.0), axis=0, keepdims=True)
    k2 = jnp.where(valid, k2, 1.0)
    norm = jnp.sqrt(q2) * jnp.sqrt(k2)
    gram_n = jnp.where(valid, t / norm, 0.0)
    datt = jnp.where(valid, pltpu.roll(t, LANES - head, 1), 0.0)
    logit = jnp.where(valid, tau * gram_n, -1e30)
    ex = jnp.exp(logit - jnp.max(logit, axis=1, keepdims=True))
    ex = jnp.where(valid, ex, 0.0)
    att = ex / jnp.sum(ex, axis=1, keepdims=True)
    d_logit = att * (datt - jnp.sum(att * datt, axis=1, keepdims=True))
    d_tau = jnp.sum(jnp.sum(d_logit * gram_n, axis=1, keepdims=True), axis=0, keepdims=True)
    e_mat = tau * d_logit
    d_gram = (e_mat / norm).astype(BF16).astype(F32)
    es = e_mat * gram_n
    q_coef = -jnp.sum(es, axis=1, keepdims=True) / q2
    k_coef = -jnp.sum(es, axis=0, keepdims=True) / k2
    k_coef = jnp.sum(jnp.where(eye, k_coef, 0.0), axis=1, keepdims=True)
    v = jnp.where(valid, att.astype(BF16).astype(F32), pltpu.roll(d_gram, head, 1))
    v = jnp.where(lane == 2 * head, q_coef, v)
    v = jnp.where(lane == 2 * head + 1, k_coef, v)
    return jnp.where(lane == 2 * head + 2, d_tau, v)


def front_kernel(tp, sp, steps, x_ref, g_ref, w_ref, w4_ref, gam_ref, bet_ref, temp_ref,
                 save_ref, wt_ref, wn_ref, wo_ref, wot_ref, m1_ref, m2_ref, cq_ref, ck_ref, dt_ref,
                 wq, gam, bet, xt, gt, ut, qd, kv, acc, sq, wall, sums, pair, parts, state, big,
                 send_w, recv_w, send_p, recv_p, send_a, recv_a, send_b, recv_b):
    step = pl.program_id(0)
    my_sp, my_tp = lax.axis_index("sp"), lax.axis_index("tp")
    chips = sp // 2
    core, chip = lax.rem(my_sp, 2), my_sp // 2
    rows, d = x_ref.shape
    own = w4_ref.shape[0]
    head = own // 2
    rest = d - own
    other = {"sp": chip * 2 + 1 - core}
    chip_peers = [{"sp": lax.rem(chip + k, chips) * 2 + core} for k in range(1, chips)]
    tp_peers = [[{"tp": lax.rem(my_tp + k, tp), "sp": chip * 2 + t} for t in range(2)] for k in range(1, tp)]
    barrier = pltpu.get_barrier_semaphore()
    peers = [other] + chip_peers + [p for ps in tp_peers for p in ps]

    @pl.when(step == 0)
    def _():
        for peer in peers:
            pl.semaphore_signal(barrier, inc=1, device_id=peer, device_id_type=MESH)
        for e in range(3):
            wq[e * own : (e + 1) * own, :] = w_ref[e]
        spread_columns(gam_ref, gam)
        spread_columns(bet_ref, bet)
        acc[...] = jnp.zeros_like(acc)
        sq[...] = jnp.zeros_like(sq)
        big[...] = jnp.zeros_like(big)

    def weight_copies():
        out = []
        for k in range(1, tp):
            for i, (src, dst) in enumerate(((w_ref, wall.at[tp - k, 0:3]), (w4_ref, wall.at[tp - k, 3]))):
                peer = {"tp": lax.rem(my_tp + k, tp), "sp": my_sp}
                out.append(remote(src, dst, send_w.at[k, i], recv_w.at[k, i], peer))
        return out

    @pl.when(step == 1)
    def _():
        pl.semaphore_wait(barrier, len(peers))
        for c in weight_copies():
            c.start()

    tiles = rows // NT
    at = lambda n: pl.ds(n * NT, NT)

    def norm(n):
        xt[:, at(n)] = x_ref[at(n), :].T
        gt[:, at(n)] = g_ref[at(n), :].T
        mean, inv = ln_stats(xt, at(n))
        mean = mean * inv
        for c in range(0, d, CH):
            v = xt[c : c + CH, at(n)].astype(F32) * inv - mean
            ut[c : c + CH, at(n)] = (v * gam[c : c + CH, :] + bet[c : c + CH, :]).astype(BF16)

    def project(n):
        qkv = dot(wq[...], ut[:, at(n)])
        for e, ref in enumerate((qd, kv)):
            v = qkv[e * own : (e + 1) * own].astype(BF16)
            ref[0:own, at(n)] = v
            save_ref[e * own : (e + 1) * own, at(n)] = v
            v = v.astype(F32)
            v = v * v
            sq[e] += v[:, :128] + v[:, 128:]
        v = qkv[2 * own :].astype(BF16)
        kv[own:, at(n)] = v
        save_ref[2 * own : 3 * own, at(n)] = v
        v = dot(w4_ref[...], gt[:, at(n)]).astype(BF16)
        qd[own:, at(n)] = v
        save_ref[3 * own :, at(n)] = v

    norm(0)
    for n in range(tiles):
        if n + 1 < tiles:
            norm(n + 1)
        project(n)
    acc[:, 0 : 2 * own] += dot_nt(qd[...], kv[...])

    @pl.when(step == steps - 1)
    def _():
        lane = lax.broadcasted_iota(jnp.int32, (head, LANES), 1)
        valid = lane < head
        for h in range(2):
            r = h * head
            gram = pltpu.roll(acc[r : r + head, :], 256 - r, 1)[:, :128] if r else acc[r : r + head, :][:, :128]
            datt = pltpu.roll(acc[own + r : own + r + head, :], 256 - (own + r) + head, 1)[:, :128]
            q2 = jnp.sum(sq[0, r : r + head, :], axis=1, keepdims=True)
            k2 = jnp.sum(sq[1, r : r + head, :], axis=1, keepdims=True)
            v = jnp.where(valid, gram, datt)
            v = jnp.where(lane == 2 * head, q2, v)
            sums[r : r + head, :] = jnp.where(lane == 2 * head + 1, k2, v)

        mine = pl.ds(pl.multiple_of(core * head, 8), head)
        theirs = pl.ds(pl.multiple_of((1 - core) * head, 8), head)
        first = remote(sums.at[theirs], pair, send_p.at[0], recv_p.at[0], other)
        first.start()
        for c in weight_copies():
            c.wait()
        first.wait()
        parts[chip] = sums[mine, :] + pair[...]
        copies = [
            remote(parts.at[chip], parts.at[chip], send_a.at[k], recv_a.at[k], chip_peers[k - 1]) for k in range(1, chips)
        ]
        for c in copies:
            c.start()
        pieces = [(w_ref, w4_ref)] + [(wall.at[j, 0:3], wall.at[j, 3]) for j in range(1, tp)]
        for j, (piece, piece4) in enumerate(pieces):
            for e in range(3):
                wn_ref[:, e * d + j * own : e * d + (j + 1) * own] = piece[e].T
                if j:
                    wt_ref[e * rest + (j - 1) * own : e * rest + j * own, :] = piece[e]
            wot_ref[:, j * own : (j + 1) * own] = piece4[...].T
            if j:
                wo_ref[(j - 1) * own : j * own, :] = piece4[...]
        for c in copies:
            c.wait()
        total = parts[0]
        for k in range(1, chips):
            total = total + parts[k]
        state[0, core] = head_state(total, temp_ref[my_tp * 2 + core], head)

        copies = [remote(state.at[0, core], state.at[0, core], send_b.at[0, 0], recv_b.at[0, core], other)]
        for k in range(1, tp):
            for t in range(2):
                copies.append(
                    remote(state.at[0, core], state.at[tp - k, core], send_b.at[k, t], recv_b.at[k, core], tp_peers[k - 1][t])
                )
        for c in copies:
            c.start()
        for c in copies:
            c.wait_send()
        remote(state.at[0, core], state.at[0, 1 - core], send_b.at[0, 0], recv_b.at[0, 1 - core], other).wait_recv()
        for k in range(1, tp):
            for t in range(2):
                remote(state.at[0, core], state.at[tp - k, t], send_b.at[k, t], recv_b.at[k, t], tp_peers[k - 1][t]).wait_recv()

        lane1 = lax.broadcasted_iota(jnp.int32, dt_ref.shape, 1)
        dt = jnp.zeros(dt_ref.shape, F32)
        zero = jnp.zeros((head, d - LANES), F32)
        for j in range(tp):
            for h in range(2):
                t = state[j, h]
                pick = lambda i: jnp.sum(jnp.where(lane == i, t, 0.0), axis=1, keepdims=True)
                r = j * own + h * head
                att = jnp.concatenate([jnp.where(valid, t, 0.0), zero], axis=1)
                d_gram = jnp.concatenate([jnp.where(valid, pltpu.roll(t, LANES - head, 1), 0.0), zero], axis=1)
                big[0, r : r + head, :] = pltpu.roll(att, r, 1) if r else att
                big[1, r : r + head, :] = pltpu.roll(d_gram, r, 1) if r else d_gram
                cq_ref[r : r + head, :] = jnp.broadcast_to(pick(2 * head), (head, NT))
                ck_ref[r : r + head, :] = jnp.broadcast_to(pick(2 * head + 1), (head, NT))
                which = lax.rem(my_tp + j, tp) * 2 + h
                dt = jnp.where(lane1 == which, pick(2 * head + 2)[0:1, :], dt)
        dt_ref[...] = dt
        low = m1_ref.shape[1]
        for i in range(2):
            m = big[i].astype(BF16)
            mt = m.T
            m1_ref[2 * i] = m[0:low, 0:256]
            m2_ref[2 * i] = m[low:, 128:]
            m1_ref[2 * i + 1] = mt[0:low, 0:256]
            m2_ref[2 * i + 1] = mt[low:, 128:]


def front_call(x, g, w, w4, gam, bet, temps, tp, sp, block=2048):
    rows, d = x.shape
    own = w4.shape[0]
    head = d // temps.shape[0]
    low = 256 // head * head
    steps = rows // block
    row = pl.BlockSpec((block, d), lambda i: (i, 0))
    full = lambda shape: pl.BlockSpec(shape, lambda i: (0,) * len(shape))
    smalls = [
        ((3 * (d - own), d), BF16),
        ((d, 3 * d), BF16),
        ((d - own, d), BF16),
        ((d, d), BF16),
        ((4, low, 256), BF16),
        ((4, d - low, 256), BF16),
        ((d, NT), F32),
        ((d, NT), F32),
        ((1, LANES), F32),
    ]
    dma = pltpu.SemaphoreType.DMA
    return pl.pallas_call(
        functools.partial(front_kernel, tp, sp, steps),
        grid=(steps,),
        in_specs=[row, row, full(w.shape), full(w4.shape), full(gam.shape), full(bet.shape), pl.BlockSpec(memory_space=pltpu.SMEM)],
        out_specs=[pl.BlockSpec((4 * own, block), lambda i: (0, i))] + [full(s) for s, _ in smalls],
        out_shape=[jax.ShapeDtypeStruct((4 * own, rows), BF16)] + [jax.ShapeDtypeStruct(s, t) for s, t in smalls],
        scratch_shapes=[
            pltpu.VMEM((3 * own, d), BF16),
            pltpu.VMEM((d, NT), F32),
            pltpu.VMEM((d, NT), F32),
            pltpu.VMEM((d, block), BF16),
            pltpu.VMEM((d, block), BF16),
            pltpu.VMEM((d, block), BF16),
            pltpu.VMEM((2 * own, block), BF16),
            pltpu.VMEM((2 * own, block), BF16),
            pltpu.VMEM((2 * own, 256), F32),
            pltpu.VMEM((2, own, 128), F32),
            pltpu.VMEM((tp, 4, own, d), BF16),
            pltpu.VMEM((own, LANES), F32),
            pltpu.VMEM((head, LANES), F32),
            pltpu.VMEM((sp // 2, head, LANES), F32),
            pltpu.VMEM((tp, 2, head, LANES), F32),
            pltpu.VMEM((2, d, d), F32),
            dma((tp, 2)),
            dma((tp, 2)),
            dma((1,)),
            dma((1,)),
            dma((sp // 2,)),
            dma((sp // 2,)),
            dma((tp, 2)),
            dma((tp, 2)),
        ],
        compiler_params=pltpu.CompilerParams(
            dimension_semantics=("arbitrary",), vmem_limit_bytes=60 * 2**20, collective_id=0, has_side_effects=True
        ),
        cost_estimate=pl.CostEstimate(flops=2 * rows * d * 4 * own, bytes_accessed=4 * rows * d, transcendentals=0),
        name="front",
    )(x, g, w, w4, gam, bet, temps)


def main_kernel(steps, x_ref, g_ref, save_ref, wt, wn, wo, wot, m1, m2, gam_ref, bet_ref, cq, ck, y_ref, dx_ref, dw_ref,
                gam, bet, xt, ut, xh, qkv, do, ot, rt, gx, inv_s, acc_w, acc_o, acc_g):
    step = pl.program_id(0)
    rows, d = x_ref.shape
    rest = wo.shape[0]
    own = d - rest
    low = m1.shape[1]

    @pl.when(step == 0)
    def _():
        spread_columns(gam_ref, gam)
        spread_columns(bet_ref, bet)
        acc_w[...] = jnp.zeros_like(acc_w)
        acc_o[...] = jnp.zeros_like(acc_o)
        acc_g[...] = jnp.zeros_like(acc_g)

    tiles = rows // NT
    at = lambda n: pl.ds(n * NT, NT)

    def norm(n):
        xt[:, at(n)] = x_ref[at(n), :].T
        mean, inv = ln_stats(xt, at(n))
        inv_s[:, at(n)] = jnp.broadcast_to(inv, (8, NT))
        mean = mean * inv
        for c in range(0, d, CH):
            v = xt[c : c + CH, at(n)].astype(F32) * inv - mean
            xh[c : c + CH, at(n)] = v
            ut[c : c + CH, at(n)] = (v * gam[c : c + CH, :] + bet[c : c + CH, :]).astype(BF16)

    def project(n):
        for e in range(3):
            qkv[e * d : e * d + own, at(n)] = save_ref[e * own : (e + 1) * own, at(n)]
            qkv[e * d + own : (e + 1) * d, at(n)] = dot(wt[e * rest : (e + 1) * rest, :], ut[:, at(n)]).astype(BF16)
        do[0:own, at(n)] = save_ref[3 * own :, at(n)]
        do[own:, at(n)] = dot_nt(wo[...], g_ref[at(n), :]).astype(BF16)

    def mix(n):
        ot[0:low, at(n)] = dot(m1[0], qkv[2 * d : 2 * d + 256, at(n)]).astype(BF16)
        ot[low:d, at(n)] = dot(m2[0], qkv[2 * d + 128 : 3 * d, at(n)]).astype(BF16)
        rt[2 * d : 2 * d + low, at(n)] = dot(m1[1], do[0:256, at(n)]).astype(BF16)
        rt[2 * d + low : 3 * d, at(n)] = dot(m2[1], do[128:d, at(n)]).astype(BF16)
        for part, other, coef, i in ((0, d, cq, 2), (d, 0, ck, 3)):
            v = dot(m1[i], qkv[other : other + 256, at(n)])
            rt[part : part + low, at(n)] = (v + qkv[part : part + low, at(n)].astype(F32) * coef[0:low, :]).astype(BF16)
            v = dot(m2[i], qkv[other + 128 : other + d, at(n)])
            rt[part + low : part + d, at(n)] = (v + qkv[part + low : part + d, at(n)].astype(F32) * coef[low:d, :]).astype(BF16)

    def out(n):
        for c, m in ((0, 128), (128, 256)):
            yt = dot(wot[c : c + m, :], ot[:, at(n)]) + xt[c : c + m, at(n)].astype(F32)
            y_ref[at(n), c : c + m] = yt.astype(BF16).T
        gx[:, at(n)] = dot(wn[...], rt[:, at(n)])

    def norm_bwd(n):
        s1 = jnp.zeros((8, NT), F32)
        s2 = jnp.zeros((8, NT), F32)
        for c in range(0, d, CH):
            du = gx[c : c + CH, at(n)]
            h = xh[c : c + CH, at(n)]
            acc_g[0, c : c + CH, :] += du * h
            acc_g[1, c : c + CH, :] += du
            a = du * gam[c : c + CH, :]
            s1 = s1 + fold8(a)
            s2 = s2 + fold8(a * h)
            gx[c : c + CH, at(n)] = a
        mean1 = jnp.sum(s1, axis=0, keepdims=True) * (1.0 / d)
        mean2 = jnp.sum(s2, axis=0, keepdims=True) * (1.0 / d)
        inv = inv_s[0:1, at(n)]
        for c in range(0, d, CH):
            v = inv * (gx[c : c + CH, at(n)] - mean1 - xh[c : c + CH, at(n)] * mean2)
            gx[c : c + CH, at(n)] = v
        dxt = gx[:, at(n)] + g_ref[at(n), :].T.astype(F32)
        dx_ref[at(n), :] = dxt.astype(BF16).T

    stages = (norm, project, mix, out, norm_bwd)
    for n in range(tiles + len(stages) - 1):
        for k in reversed(range(len(stages))):
            if 0 <= n - k < tiles:
                stages[k](n - k)
    r_own = jnp.concatenate([rt[e * d : e * d + own, :] for e in range(3)], axis=0)
    acc_w[...] += dot_nt(r_own, ut[...])
    acc_o[...] += dot(ot[0:own, :], g_ref[...])

    @pl.when(step == steps - 1)
    def _():
        sp, slot_rows = dw_ref.shape[0], dw_ref.shape[1]
        per = d // sp
        sub = own // sp
        wgrad = acc_w[...].T
        for s in range(sp):
            dw_ref[s, 0:per, 0 : 3 * own] = wgrad[s * per : (s + 1) * per, :]
            for q in range(d // own):
                dw_ref[s, q * sub : (q + 1) * sub, 3 * own :] = acc_o[s * sub : (s + 1) * sub, q * own : (q + 1) * own]
        zero = jnp.zeros((slot_rows - per - 2, d), F32)
        gb = jnp.concatenate([jnp.sum(acc_g[i].T, axis=0, keepdims=True) for i in range(2)] + [zero], axis=0)
        for s in range(sp):
            dw_ref[s, per:slot_rows, :] = gb


def main_call(x, g, save, wt, wn, wo, wot, m1, m2, gam, bet, cq, ck, sp, block=2048):
    rows, d = x.shape
    own = d - wo.shape[0]
    steps = rows // block
    row = pl.BlockSpec((block, d), lambda i: (i, 0))
    full = lambda a: pl.BlockSpec(a.shape, lambda i: (0,) * a.ndim)
    slot = (sp, d // sp + 8, d)
    smalls = (wt, wn, wo, wot, m1, m2, gam, bet, cq, ck)
    return pl.pallas_call(
        functools.partial(main_kernel, steps),
        grid=(steps,),
        in_specs=[row, row, pl.BlockSpec((4 * own, block), lambda i: (0, i))] + [full(a) for a in smalls],
        out_specs=[row, row, pl.BlockSpec(slot, lambda i: (0, 0, 0))],
        out_shape=[jax.ShapeDtypeStruct((rows, d), BF16), jax.ShapeDtypeStruct((rows, d), BF16), jax.ShapeDtypeStruct(slot, F32)],
        scratch_shapes=[
            pltpu.VMEM((d, NT), F32),
            pltpu.VMEM((d, NT), F32),
            pltpu.VMEM((d, block), BF16),
            pltpu.VMEM((d, block), BF16),
            pltpu.VMEM((d, block), F32),
            pltpu.VMEM((3 * d, block), BF16),
            pltpu.VMEM((d, block), BF16),
            pltpu.VMEM((d, block), BF16),
            pltpu.VMEM((3 * d, block), BF16),
            pltpu.VMEM((d, block), F32),
            pltpu.VMEM((8, block), F32),
            pltpu.VMEM((3 * own, d), F32),
            pltpu.VMEM((own, d), F32),
            pltpu.VMEM((2, d, NT), F32),
        ],
        compiler_params=pltpu.CompilerParams(dimension_semantics=("arbitrary",), vmem_limit_bytes=60 * 2**20),
        cost_estimate=pl.CostEstimate(flops=2 * rows * d * d * 9, bytes_accessed=8 * rows * d, transcendentals=0),
        name="main",
    )(x, g, save, *smalls)


def wgrad_kernel(sp, in_ref, w_ref, o_ref, gam_ref, bet_ref, pair, got, send_a, recv_a, send_b, recv_b):
    my = lax.axis_index("sp")
    chips = sp // 2
    core, chip = lax.rem(my, 2), my // 2
    other = {"sp": chip * 2 + 1 - core}
    peers = [{"sp": lax.rem(chip + k, chips) * 2 + core} for k in range(1, chips)]
    barrier = pltpu.get_barrier_semaphore()
    for peer in [other] + peers:
        pl.semaphore_signal(barrier, inc=1, device_id=peer, device_id_type=MESH)
    pl.semaphore_wait(barrier, chips)
    first = [remote(in_ref.at[2 * c + 1 - core], pair.at[c], send_a.at[c], recv_a.at[c], other) for c in range(chips)]
    for c in first:
        c.start()
    for c in range(chips):
        first[c].wait()
    for c in range(chips):
        got[chips + c] = in_ref[2 * c + core] + pair[c]
    second = [
        remote(got.at[chips + lax.rem(chip + k, chips)], got.at[chip], send_b.at[k], recv_b.at[k], peers[k - 1])
        for k in range(1, chips)
    ]
    for c in second:
        c.start()
    got[chip] = got[chips + chip]
    for c in second:
        c.wait()
    total = got[0]
    for c in range(1, chips):
        total = total + got[c]
    per, own = w_ref.shape[1:]
    sub = o_ref.shape[0]
    for e in range(3):
        w_ref[e] = total[0:per, e * own : (e + 1) * own]
    for q in range(o_ref.shape[1] // own):
        o_ref[:, q * own : (q + 1) * own] = total[q * sub : (q + 1) * sub, 3 * own :]
    gam_ref[...] = total[per]
    bet_ref[...] = total[per + 1]


def wgrad_call(parts, own):
    sp, rows, d = parts.shape
    vmem = pl.BlockSpec(memory_space=pltpu.VMEM)
    return pl.pallas_call(
        functools.partial(wgrad_kernel, sp),
        in_specs=[vmem],
        out_specs=[vmem] * 4,
        out_shape=[
            jax.ShapeDtypeStruct((3, d // sp, own), F32),
            jax.ShapeDtypeStruct((own // sp, d), F32),
            jax.ShapeDtypeStruct((d,), F32),
            jax.ShapeDtypeStruct((d,), F32),
        ],
        scratch_shapes=[
            pltpu.VMEM((sp // 2, rows, d), F32),
            pltpu.VMEM((sp, rows, d), F32),
            pltpu.SemaphoreType.DMA((sp // 2,)),
            pltpu.SemaphoreType.DMA((sp // 2,)),
            pltpu.SemaphoreType.DMA((sp // 2,)),
            pltpu.SemaphoreType.DMA((sp // 2,)),
        ],
        compiler_params=pltpu.CompilerParams(collective_id=1, has_side_effects=True),
        name="wgrad",
    )(parts)


def solution(mesh):
    tp, sp = mesh.shape["tp"], mesh.shape["sp"]
    row_spec = P(("dp", "sp"), None)

    def local_step(x, g, w_qkv, w_out, gamma, beta, temps):
        save, wt, wn, wo, wot, m1, m2, cq, ck, dt = front_call(
            x, g, w_qkv.transpose(1, 2, 0), w_out, gamma, beta, temps, tp, sp
        )
        y, dx, parts = main_call(x, g, save, wt, wn, wo, wot, m1, m2, gamma, beta, cq, ck, sp)
        grad_w, grad_o, grad_gamma, grad_beta = wgrad_call(parts, w_out.shape[0])
        return y, dx, grad_w.transpose(1, 0, 2), grad_o, grad_gamma, grad_beta, dt[0, : temps.shape[0]]

    in_specs = (row_spec, row_spec, P(None, None, "tp"), P("tp", None), P(None), P(None), P(None))
    out_specs = (row_spec, row_spec, P(("dp", "sp"), None, "tp"), P(("dp", "tp", "sp"), None), P("dp"), P("dp"), P("dp"))
    return jax.shard_map(local_step, mesh=mesh, in_specs=in_specs, out_specs=out_specs, check_vma=False)
```

time: 1030 us -> 142 us (0.14)
  waiting for transfers between devices: 774 us -> 0 us
  Pallas kernels: 0 us -> 135 us
  matrix products: 84.6 us -> 0 us
  other arithmetic: 71.9 us -> 0 us
  blocking collectives: 68.8 us -> 0 us
  between operations: 17.1 us -> 0.66 us
    psum x1 -> x0, waiting for transfers between devices: 774 us -> none  [local_step(): lax.psum(y_part, 'tp')]
    pallas_call x0 -> x3, Pallas kernels: none -> 135 us  [the longest x1 83.1 us: main_call(): pl.pallas_call(functools.partial(main_kernel, steps), grid=(steps,), in_s...]
    dot_general x11 -> x0, matrix products: 77.9 us -> none  [the longest x1 16.4 us: local_step(): jnp.einsum('nd,nec->dec', u_act, dqkv_act, preferred_element_type=jnp.flo...]
    psum x2 -> x0, blocking collectives: 39.8 us -> none  [the longest x1 26.5 us: local_step(): gram_mat, q_sq, k_sq = lax.psum((gram_part, q_part, k_part), 'sp')]
    convert_element_type x2 -> x0, other arithmetic: 33.7 us -> none  [the longest x1 32.7 us: local_step(): (grad_blk.astype(jnp.float32) + layer_norm_bwd(grad_u, x_hat, inv_std, ln...]
    reduce_sum x3 -> x0, other arithmetic: 32.6 us -> none  [the longest x1 17.8 us: local_step(): jnp.sum(grad_u * x_hat, axis=0)]
    unnamed x2 -> x0, blocking collectives: 29 us -> none
  transfers between devices with their start and end apart: 4 -> 0, of which waited for: 1 -> 0; matrix products, arithmetic and copies ran while one was open for 9% -> 0% of each run, Pallas kernels for 0% -> 0%
where the time goes in v2:
time: 142 us
  Pallas kernels  135 us (95%)
  local copies, waits for them, and re-layouts  6.46 us (5%)
    pallas_call x1, Pallas kernels, main_call(): pl.pallas_call(functools.partial(main_kernel, steps), grid=(steps,), in_s...  83.1 us
    pallas_call x1, Pallas kernels, front_call(): pl.pallas_call(functools.partial(front_kernel, tp, sp, steps), grid=(step...  40.5 us
    pallas_call x1, Pallas kernels, wgrad_call(): pl.pallas_call(functools.partial(wgrad_kernel, sp), in_specs=[vmem], out_...  11.4 us
    unnamed x4, local copies, waits for them, and re-layouts  5.34 us

profile of v2, /device:TPU:97, one launch (start us, length us, event | category | flops | bytes accessed | tf_op | source)
XLA Modules:
  0.0 142.1 jit_solution(7515829434636506463)
XLA Ops:
  0.6 40.5 %front.1 = (bf16[384,16384]{1,0:T(8,128)(2,1)}, bf16[864,384]{1,0:T(8,128)(2,1)}, bf16[384,1152]{1,0:T(8,128)(2,1)}, bf16[288,384]{1,0:T(8,128)(2,1)}, bf16[384,...) custom-call(bf16[16384,384]{1,0:T(8,128)(2,1)} %x_ref.3, ...), custom_call_target="tpu_custom_call" | custom-call | flops 4831838208 | bytes 25165824 | tf_op jit(solution)/shard_map/front/pallas_call | solution.py:269
  41.1 1.1 slice_bitcast_fusion
  42.2 83.1 %main.1 = (bf16[16384,384]{1,0:T(8,128)(2,1)}, bf16[16384,384]{1,0:T(8,128)(2,1)}, f32[8,56,384]{2,1,0:T(8,128)}) custom-call(bf16[16384,384]{1,0:T(8,128)(2,1)} %x_ref.3, bf16[16384,384]{1,0:T(8,128)(2,1)} %g_ref.3, bf16[384,16384]{1,0:T(8,128)(2,1)} %get-tuple-element.24.save_ref, bf16[864,384]{1,0:T(8,128)(2,1)} %get-tuple-element.25.wt, ...), custom_call_target="tpu_custom_call" | custom-call | flops 43486543872 | bytes 50331648 | tf_op jit(solution)/shard_map/main/pallas_call | solution.py:416
  125.4 11.4 %wgrad.1 = (f32[3,48,96]{2,1,0:T(8,128)}, f32[12,384]{1,0:T(8,128)}, f32[384]{0:T(512)}, f32[384]{0:T(512)}) custom-call(f32[8,56,384]{2,1,0:T(8,128)} %get-tuple-element.35.in_ref), custom_call_target="tpu_custom_call" | custom-call | tf_op jit(solution)/shard_map/wgrad/pallas_call | solution.py:486
  136.8 1.5 %copy.18 = f32[48,3,96]{2,0,1:T(8,128)} copy(f32[48,3,96]{2,0,1:T(8,128)} %bitcast.5) | data formatting | bytes 110592
  138.3 1.3 copy.19
  139.7 1.2 copy.20
  140.9 1.2 copy.21

commit v3 on v2

--- a/solution.py
+++ b/solution.py
@@ -83,9 +83,9 @@
 
 
 def front_kernel(tp, sp, steps, x_ref, g_ref, w_ref, w4_ref, gam_ref, bet_ref, temp_ref,
-                 save_ref, wt_ref, wn_ref, wo_ref, wot_ref, m1_ref, m2_ref, cq_ref, ck_ref, dt_ref,
-                 wq, gam, bet, xt, gt, ut, qd, kv, acc, sq, wall, sums, pair, parts, state, big,
-                 send_w, recv_w, send_p, recv_p, send_a, recv_a, send_b, recv_b):
+                 save_ref, u_ref, st_ref, wt_ref, wn_ref, wo_ref, wot_ref, m1_ref, m2_ref, cq_ref, ck_ref, dt_ref,
+                 wq, gam, bet, xt, gt, ut, save_s, u_s, qd, kv, acc, sq, wall, sums, pair, parts, state, big,
+                 out_sem, send_w, recv_w, send_p, recv_p, send_a, recv_a, send_b, recv_b):
     step = pl.program_id(0)
     my_sp, my_tp = lax.axis_index("sp"), lax.axis_index("tp")
     chips = sp // 2
@@ -126,6 +126,20 @@
         for c in weight_copies():
             c.start()
 
+    slot = lax.rem(step, 2)
+
+    def save_copies(to, at_slot):
+        cols = pl.ds(pl.multiple_of(to * rows, LANES), rows)
+        return [
+            pltpu.make_async_copy(save_s.at[at_slot], save_ref.at[:, cols], out_sem.at[at_slot, 0]),
+            pltpu.make_async_copy(u_s.at[at_slot], u_ref.at[:, cols], out_sem.at[at_slot, 1]),
+        ]
+
+    @pl.when(step >= 2)
+    def _():
+        for c in save_copies(step - 2, slot):
+            c.wait()
+
     tiles = rows // NT
     at = lambda n: pl.ds(n * NT, NT)
 
@@ -134,44 +148,60 @@
         gt[:, at(n)] = g_ref[at(n), :].T
         mean, inv = ln_stats(xt, at(n))
         mean = mean * inv
+        st_ref[0:1, at(n)] = mean
+        st_ref[1:2, at(n)] = inv
         for c in range(0, d, CH):
             v = xt[c : c + CH, at(n)].astype(F32) * inv - mean
-            ut[c : c + CH, at(n)] = (v * gam[c : c + CH, :] + bet[c : c + CH, :]).astype(BF16)
+            v = (v * gam[c : c + CH, :] + bet[c : c + CH, :]).astype(BF16)
+            ut[c : c + CH, at(n)] = v
+            u_s[slot, c : c + CH, at(n)] = v
 
     def project(n):
         qkv = dot(wq[...], ut[:, at(n)])
-        for e, ref in enumerate((qd, kv)):
+        for e, (ref, r) in enumerate(((qd, 0), (kv, 0), (kv, own))):
             v = qkv[e * own : (e + 1) * own].astype(BF16)
-            ref[0:own, at(n)] = v
-            save_ref[e * own : (e + 1) * own, at(n)] = v
-            v = v.astype(F32)
-            v = v * v
-            sq[e] += v[:, :128] + v[:, 128:]
-        v = qkv[2 * own :].astype(BF16)
-        kv[own:, at(n)] = v
-        save_ref[2 * own : 3 * own, at(n)] = v
+            ref[r : r + own, at(n)] = v
+            save_s[slot, e * own : (e + 1) * own, at(n)] = v
+            if e == 0:
+                v = v.astype(F32)
+                v = v * v
+                sq[...] += v[:, :LANES] + v[:, LANES:]
         v = dot(w4_ref[...], gt[:, at(n)]).astype(BF16)
         qd[own:, at(n)] = v
-        save_ref[3 * own :, at(n)] = v
+        save_s[slot, 3 * own :, at(n)] = v
+
+    def gram(n):
+        cols = pl.ds(n * NT, 2 * NT)
+        left = jnp.concatenate([qd[:, cols], kv[0:own, cols]], axis=0)
+        acc[:, 0 : 2 * own] += dot_nt(left, kv[:, cols])
 
     norm(0)
     for n in range(tiles):
         if n + 1 < tiles:
             norm(n + 1)
+        if n >= 2 and n % 2 == 0:
+            gram(n - 2)
         project(n)
-    acc[:, 0 : 2 * own] += dot_nt(qd[...], kv[...])
+    gram(tiles - 2)
+    for c in save_copies(step, slot):
+        c.start()
 
     @pl.when(step == steps - 1)
     def _():
         lane = lax.broadcasted_iota(jnp.int32, (head, LANES), 1)
+        row = lax.broadcasted_iota(jnp.int32, (head, LANES), 0)
         valid = lane < head
+
+        def block(r, c, to):
+            shift = (to - c) % 256
+            v = acc[r : r + head, :]
+            return (pltpu.roll(v, shift, 1) if shift else v)[:, :LANES]
+
         for h in range(2):
             r = h * head
-            gram = pltpu.roll(acc[r : r + head, :], 256 - r, 1)[:, :128] if r else acc[r : r + head, :][:, :128]
-            datt = pltpu.roll(acc[own + r : own + r + head, :], 256 - (own + r) + head, 1)[:, :128]
-            q2 = jnp.sum(sq[0, r : r + head, :], axis=1, keepdims=True)
-            k2 = jnp.sum(sq[1, r : r + head, :], axis=1, keepdims=True)
-            v = jnp.where(valid, gram, datt)
+            q2 = jnp.sum(sq[r : r + head, :], axis=1, keepdims=True)
+            k2 = jnp.sum(jnp.where(lane == row, block(2 * own + r, r, 0), 0.0), axis=1, keepdims=True)
+            v = jnp.where(valid, block(r, r, 0), block(own + r, own + r, head))
             v = jnp.where(lane == 2 * head, q2, v)
             sums[r : r + head, :] = jnp.where(lane == 2 * head + 1, k2, v)
 
@@ -244,6 +274,8 @@
             m2_ref[2 * i] = m[low:, 128:]
             m1_ref[2 * i + 1] = mt[0:low, 0:256]
             m2_ref[2 * i + 1] = mt[low:, 128:]
+        for c in save_copies(step - 1, 1 - slot) + save_copies(step, slot):
+            c.wait()
 
 
 def front_call(x, g, w, w4, gam, bet, temps, tp, sp, block=2048):
@@ -270,8 +302,10 @@
         functools.partial(front_kernel, tp, sp, steps),
         grid=(steps,),
         in_specs=[row, row, full(w.shape), full(w4.shape), full(gam.shape), full(bet.shape), pl.BlockSpec(memory_space=pltpu.SMEM)],
-        out_specs=[pl.BlockSpec((4 * own, block), lambda i: (0, i))] + [full(s) for s, _ in smalls],
-        out_shape=[jax.ShapeDtypeStruct((4 * own, rows), BF16)] + [jax.ShapeDtypeStruct(s, t) for s, t in smalls],
+        out_specs=[pl.BlockSpec(memory_space=pl.ANY)] * 2
+        + [pl.BlockSpec((8, block), lambda i: (0, i))]
+        + [full(s) for s, _ in smalls],
+        out_shape=[jax.ShapeDtypeStruct((r, rows), t) for r, t in ((4 * own, BF16), (d, BF16), (8, F32))] + [jax.ShapeDtypeStruct(s, t) for s, t in smalls],
         scratch_shapes=[
             pltpu.VMEM((3 * own, d), BF16),
             pltpu.VMEM((d, NT), F32),
@@ -279,16 +313,19 @@
             pltpu.VMEM((d, block), BF16),
             pltpu.VMEM((d, block), BF16),
             pltpu.VMEM((d, block), BF16),
+            pltpu.VMEM((2, 4 * own, block), BF16),
+            pltpu.VMEM((2, d, block), BF16),
             pltpu.VMEM((2 * own, block), BF16),
             pltpu.VMEM((2 * own, block), BF16),
-            pltpu.VMEM((2 * own, 256), F32),
-            pltpu.VMEM((2, own, 128), F32),
+            pltpu.VMEM((3 * own, 256), F32),
+            pltpu.VMEM((own, LANES), F32),
             pltpu.VMEM((tp, 4, own, d), BF16),
             pltpu.VMEM((own, LANES), F32),
             pltpu.VMEM((head, LANES), F32),
             pltpu.VMEM((sp // 2, head, LANES), F32),
             pltpu.VMEM((tp, 2, head, LANES), F32),
             pltpu.VMEM((2, d, d), F32),
+            dma((2, 2)),
             dma((tp, 2)),
             dma((tp, 2)),
             dma((1,)),
@@ -306,8 +343,8 @@
     )(x, g, w, w4, gam, bet, temps)
 
 
-def main_kernel(steps, x_ref, g_ref, save_ref, wt, wn, wo, wot, m1, m2, gam_ref, bet_ref, cq, ck, y_ref, dx_ref, dw_ref,
-                gam, bet, xt, ut, xh, qkv, do, ot, rt, gx, inv_s, acc_w, acc_o, acc_g):
+def main_kernel(steps, x_ref, g_ref, save_ref, u_ref, st_ref, wt, wn, wo, wot, m1, m2, gam_ref, cq, ck, y_ref, dx_ref, dw_ref,
+                gam, xt, gt, qkv, do, ot, rt, gx, acc_w, acc_o, acc_g):
     step = pl.program_id(0)
     rows, d = x_ref.shape
     rest = wo.shape[0]
@@ -317,7 +354,6 @@
     @pl.when(step == 0)
     def _():
         spread_columns(gam_ref, gam)
-        spread_columns(bet_ref, bet)
         acc_w[...] = jnp.zeros_like(acc_w)
         acc_o[...] = jnp.zeros_like(acc_o)
         acc_g[...] = jnp.zeros_like(acc_g)
@@ -325,20 +361,10 @@
     tiles = rows // NT
     at = lambda n: pl.ds(n * NT, NT)
 
-    def norm(n):
-        xt[:, at(n)] = x_ref[at(n), :].T
-        mean, inv = ln_stats(xt, at(n))
-        inv_s[:, at(n)] = jnp.broadcast_to(inv, (8, NT))
-        mean = mean * inv
-        for c in range(0, d, CH):
-            v = xt[c : c + CH, at(n)].astype(F32) * inv - mean
-            xh[c : c + CH, at(n)] = v
-            ut[c : c + CH, at(n)] = (v * gam[c : c + CH, :] + bet[c : c + CH, :]).astype(BF16)
-
     def project(n):
         for e in range(3):
             qkv[e * d : e * d + own, at(n)] = save_ref[e * own : (e + 1) * own, at(n)]
-            qkv[e * d + own : (e + 1) * d, at(n)] = dot(wt[e * rest : (e + 1) * rest, :], ut[:, at(n)]).astype(BF16)
+            qkv[e * d + own : (e + 1) * d, at(n)] = dot(wt[e * rest : (e + 1) * rest, :], u_ref[:, at(n)]).astype(BF16)
         do[0:own, at(n)] = save_ref[3 * own :, at(n)]
         do[own:, at(n)] = dot_nt(wo[...], g_ref[at(n), :]).astype(BF16)
 
@@ -354,39 +380,52 @@
             rt[part + low : part + d, at(n)] = (v + qkv[part + low : part + d, at(n)].astype(F32) * coef[low:d, :]).astype(BF16)
 
     def out(n):
+        xt[:, at(n)] = x_ref[at(n), :].T
         for c, m in ((0, 128), (128, 256)):
             yt = dot(wot[c : c + m, :], ot[:, at(n)]) + xt[c : c + m, at(n)].astype(F32)
             y_ref[at(n), c : c + m] = yt.astype(BF16).T
         gx[:, at(n)] = dot(wn[...], rt[:, at(n)])
 
-    def norm_bwd(n):
-        s1 = jnp.zeros((8, NT), F32)
-        s2 = jnp.zeros((8, NT), F32)
+    def norm_bwd(first):
+        pair = (first, first + 1)
+        mean = {n: st_ref[0:1, at(n)] for n in pair}
+        inv = {n: st_ref[1:2, at(n)] for n in pair}
+        s1 = {n: jnp.zeros((8, NT), F32) for n in pair}
+        s2 = {n: jnp.zeros((8, NT), F32) for n in pair}
         for c in range(0, d, CH):
-            du = gx[c : c + CH, at(n)]
-            h = xh[c : c + CH, at(n)]
-            acc_g[0, c : c + CH, :] += du * h
-            acc_g[1, c : c + CH, :] += du
-            a = du * gam[c : c + CH, :]
-            s1 = s1 + fold8(a)
-            s2 = s2 + fold8(a * h)
-            gx[c : c + CH, at(n)] = a
-        mean1 = jnp.sum(s1, axis=0, keepdims=True) * (1.0 / d)
-        mean2 = jnp.sum(s2, axis=0, keepdims=True) * (1.0 / d)
-        inv = inv_s[0:1, at(n)]
-        for c in range(0, d, CH):
-            v = inv * (gx[c : c + CH, at(n)] - mean1 - xh[c : c + CH, at(n)] * mean2)
-            gx[c : c + CH, at(n)] = v
-        dxt = gx[:, at(n)] + g_ref[at(n), :].T.astype(F32)
-        dx_ref[at(n), :] = dxt.astype(BF16).T
-
-    stages = (norm, project, mix, out, norm_bwd)
-    for n in range(tiles + len(stages) - 1):
+            gm = gam[c : c + CH, :]
+            sum_h, sum_u = [], []
+            for n in pair:
+                du = gx[c : c + CH, at(n)]
+                duh = du * (xt[c : c + CH, at(n)].astype(F32) * inv[n] - mean[n])
+                s1[n] = s1[n] + fold8(du * gm)
+                s2[n] = s2[n] + fold8(duh * gm)
+                sum_h.append(duh)
+                sum_u.append(du)
+            v = sum_h[0] + sum_h[1]
+            acc_g[0, c : c + CH, :] += v[:, :LANES] + v[:, LANES:]
+            v = sum_u[0] + sum_u[1]
+            acc_g[1, c : c + CH, :] += v[:, :LANES] + v[:, LANES:]
+        for n in pair:
+            m1_ = jnp.sum(s1[n], axis=0, keepdims=True) * (1.0 / d)
+            m2_ = jnp.sum(s2[n], axis=0, keepdims=True) * (1.0 / d)
+            slope = m2_ * inv[n] * inv[n]
+            base = inv[n] * (mean[n] * m2_ - m1_)
+            gt[:, at(n)] = g_ref[at(n), :].T
+            for c in range(0, d, CH):
+                v = gx[c : c + CH, at(n)] * gam[c : c + CH, :] * inv[n] + base - xt[c : c + CH, at(n)].astype(F32) * slope
+                gt[c : c + CH, at(n)] = (v + gt[c : c + CH, at(n)].astype(F32)).astype(BF16)
+            dx_ref[at(n), :] = gt[:, at(n)].T
+
+    stages = (project, mix, out)
+    for n in range(tiles + len(stages) + 1):
+        if n >= 4 and n % 2 == 0:
+            norm_bwd(n - 4)
         for k in reversed(range(len(stages))):
             if 0 <= n - k < tiles:
                 stages[k](n - k)
     r_own = jnp.concatenate([rt[e * d : e * d + own, :] for e in range(3)], axis=0)
-    acc_w[...] += dot_nt(r_own, ut[...])
+    acc_w[...] += dot_nt(r_own, u_ref[...])
     acc_o[...] += dot(ot[0:own, :], g_ref[...])
 
     @pl.when(step == steps - 1)
@@ -405,43 +444,41 @@
             dw_ref[s, per:slot_rows, :] = gb
 
 
-def main_call(x, g, save, wt, wn, wo, wot, m1, m2, gam, bet, cq, ck, sp, block=2048):
+def main_call(x, g, save, u, st, wt, wn, wo, wot, m1, m2, gam, cq, ck, sp, block=2048):
     rows, d = x.shape
     own = d - wo.shape[0]
     steps = rows // block
     row = pl.BlockSpec((block, d), lambda i: (i, 0))
+    col = lambda a: pl.BlockSpec((a.shape[0], block), lambda i: (0, i))
     full = lambda a: pl.BlockSpec(a.shape, lambda i: (0,) * a.ndim)
     slot = (sp, d // sp + 8, d)
-    smalls = (wt, wn, wo, wot, m1, m2, gam, bet, cq, ck)
+    smalls = (wt, wn, wo, wot, m1, m2, gam, cq, ck)
     return pl.pallas_call(
         functools.partial(main_kernel, steps),
         grid=(steps,),
-        in_specs=[row, row, pl.BlockSpec((4 * own, block), lambda i: (0, i))] + [full(a) for a in smalls],
+        in_specs=[row, row, col(save), col(u), col(st)] + [full(a) for a in smalls],
         out_specs=[row, row, pl.BlockSpec(slot, lambda i: (0, 0, 0))],
         out_shape=[jax.ShapeDtypeStruct((rows, d), BF16), jax.ShapeDtypeStruct((rows, d), BF16), jax.ShapeDtypeStruct(slot, F32)],
         scratch_shapes=[
             pltpu.VMEM((d, NT), F32),
-            pltpu.VMEM((d, NT), F32),
-            pltpu.VMEM((d, block), BF16),
-            pltpu.VMEM((d, block), BF16),
-            pltpu.VMEM((d, block), F32),
+            pltpu.VMEM((d, block), BF16),
+            pltpu.VMEM((d, block), BF16),
             pltpu.VMEM((3 * d, block), BF16),
             pltpu.VMEM((d, block), BF16),
             pltpu.VMEM((d, block), BF16),
             pltpu.VMEM((3 * d, block), BF16),
             pltpu.VMEM((d, block), F32),
-            pltpu.VMEM((8, block), F32),
             pltpu.VMEM((3 * own, d), F32),
             pltpu.VMEM((own, d), F32),
-            pltpu.VMEM((2, d, NT), F32),
+            pltpu.VMEM((2, d, LANES), F32),
         ],
         compiler_params=pltpu.CompilerParams(dimension_semantics=("arbitrary",), vmem_limit_bytes=60 * 2**20),
         cost_estimate=pl.CostEstimate(flops=2 * rows * d * d * 9, bytes_accessed=8 * rows * d, transcendentals=0),
         name="main",
-    )(x, g, save, *smalls)
-
-
-def wgrad_kernel(sp, in_ref, w_ref, o_ref, gam_ref, bet_ref, pair, got, send_a, recv_a, send_b, recv_b):
+    )(x, g, save, u, st, *smalls)
+
+
+def wgrad_kernel(sp, in_ref, out_ref, mine, pair, got, sem, send_a, recv_a, send_b, recv_b):
     my = lax.axis_index("sp")
     chips = sp // 2
     core, chip = lax.rem(my, 2), my // 2
@@ -450,14 +487,17 @@
     barrier = pltpu.get_barrier_semaphore()
     for peer in [other] + peers:
         pl.semaphore_signal(barrier, inc=1, device_id=peer, device_id_type=MESH)
+    load = pltpu.make_async_copy(in_ref, mine, sem)
+    load.start()
+    load.wait()
     pl.semaphore_wait(barrier, chips)
-    first = [remote(in_ref.at[2 * c + 1 - core], pair.at[c], send_a.at[c], recv_a.at[c], other) for c in range(chips)]
+    first = [remote(mine.at[2 * c + 1 - core], pair.at[c], send_a.at[c], recv_a.at[c], other) for c in range(chips)]
     for c in first:
         c.start()
     for c in range(chips):
         first[c].wait()
     for c in range(chips):
-        got[chips + c] = in_ref[2 * c + core] + pair[c]
+        got[chips + c] = mine[2 * c + core] + pair[c]
     second = [
         remote(got.at[chips + lax.rem(chip + k, chips)], got.at[chip], send_b.at[k], recv_b.at[k], peers[k - 1])
         for k in range(1, chips)
@@ -470,53 +510,70 @@
     total = got[0]
     for c in range(1, chips):
         total = total + got[c]
-    per, own = w_ref.shape[1:]
-    sub = o_ref.shape[0]
-    for e in range(3):
-        w_ref[e] = total[0:per, e * own : (e + 1) * own]
-    for q in range(o_ref.shape[1] // own):
-        o_ref[:, q * own : (q + 1) * own] = total[q * sub : (q + 1) * sub, 3 * own :]
-    gam_ref[...] = total[per]
-    bet_ref[...] = total[per + 1]
-
-
-def wgrad_call(parts, own):
-    sp, rows, d = parts.shape
-    vmem = pl.BlockSpec(memory_space=pltpu.VMEM)
+    out_ref[...] = total
+
+
+def wgrad_call(parts):
+    sp, slot = parts.shape[0], parts.shape[1:]
+    dma = pltpu.SemaphoreType.DMA
     return pl.pallas_call(
         functools.partial(wgrad_kernel, sp),
-        in_specs=[vmem],
-        out_specs=[vmem] * 4,
-        out_shape=[
-            jax.ShapeDtypeStruct((3, d // sp, own), F32),
-            jax.ShapeDtypeStruct((own // sp, d), F32),
-            jax.ShapeDtypeStruct((d,), F32),
-            jax.ShapeDtypeStruct((d,), F32),
-        ],
+        in_specs=[pl.BlockSpec(memory_space=pl.ANY)],
+        out_specs=pl.BlockSpec(memory_space=pltpu.VMEM),
+        out_shape=jax.ShapeDtypeStruct(slot, F32),
         scratch_shapes=[
-            pltpu.VMEM((sp // 2, rows, d), F32),
-            pltpu.VMEM((sp, rows, d), F32),
-            pltpu.SemaphoreType.DMA((sp // 2,)),
-            pltpu.SemaphoreType.DMA((sp // 2,)),
-            pltpu.SemaphoreType.DMA((sp // 2,)),
-            pltpu.SemaphoreType.DMA((sp // 2,)),
+            pltpu.VMEM((sp, *slot), F32),
+            pltpu.VMEM((sp // 2, *slot), F32),
+            pltpu.VMEM((sp, *slot), F32),
+            dma,
+            dma((sp // 2,)),
+            dma((sp // 2,)),
+            dma((sp // 2,)),
+            dma((sp // 2,)),
         ],
         compiler_params=pltpu.CompilerParams(collective_id=1, has_side_effects=True),
         name="wgrad",
     )(parts)
 
 
+def finish_kernel(sum_ref, dt_ref, w_ref, o_ref, gam_ref, bet_ref, tau_ref):
+    per, own = w_ref.shape[1:]
+    sub = o_ref.shape[0]
+    for e in range(3):
+        w_ref[e] = sum_ref[0:per, e * own : (e + 1) * own]
+    for q in range(o_ref.shape[1] // own):
+        o_ref[:, q * own : (q + 1) * own] = sum_ref[q * sub : (q + 1) * sub, 3 * own :]
+    gam_ref[...] = sum_ref[per]
+    bet_ref[...] = sum_ref[per + 1]
+    tau_ref[...] = dt_ref[0, 0 : tau_ref.shape[0]]
+
+
+def finish_call(total, dt, own, sp, heads):
+    d = total.shape[1]
+    vmem = pl.BlockSpec(memory_space=pltpu.VMEM)
+    shapes = [(3, d // sp, own), (own // sp, d), (d,), (d,), (heads,)]
+    return pl.pallas_call(
+        finish_kernel,
+        in_specs=[vmem, vmem],
+        out_specs=[vmem] * 5,
+        out_shape=[jax.ShapeDtypeStruct(s, F32) for s in shapes],
+        name="finish",
+    )(total, dt)
+
+
 def solution(mesh):
     tp, sp = mesh.shape["tp"], mesh.shape["sp"]
     row_spec = P(("dp", "sp"), None)
 
     def local_step(x, g, w_qkv, w_out, gamma, beta, temps):
-        save, wt, wn, wo, wot, m1, m2, cq, ck, dt = front_call(
+        save, u, st, wt, wn, wo, wot, m1, m2, cq, ck, dt = front_call(
             x, g, w_qkv.transpose(1, 2, 0), w_out, gamma, beta, temps, tp, sp
         )
-        y, dx, parts = main_call(x, g, save, wt, wn, wo, wot, m1, m2, gamma, beta, cq, ck, sp)
-        grad_w, grad_o, grad_gamma, grad_beta = wgrad_call(parts, w_out.shape[0])
-        return y, dx, grad_w.transpose(1, 0, 2), grad_o, grad_gamma, grad_beta, dt[0, : temps.shape[0]]
+        y, dx, parts = main_call(x, g, save, u, st, wt, wn, wo, wot, m1, m2, gamma, cq, ck, sp)
+        grad_w, grad_o, grad_gamma, grad_beta, grad_temp = finish_call(
+            wgrad_call(parts), dt, w_out.shape[0], sp, temps.shape[0]
+        )
+        return y, dx, grad_w.transpose(1, 0, 2), grad_o, grad_gamma, grad_beta, grad_temp
 
     in_specs = (row_spec, row_spec, P(None, None, "tp"), P("tp", None), P(None), P(None), P(None))
     out_specs = (row_spec, row_spec, P(("dp", "sp"), None, "tp"), P(("dp", "tp", "sp"), None), P("dp"), P("dp"), P("dp"))

time: 142 us -> 134 us (0.944)
  local copies, waits for them, and re-layouts: 6.46 us -> 0 us
  Pallas kernels: 135 us -> 133 us
    unnamed x4 -> x0, local copies, waits for them, and re-layouts: 5.34 us -> none
    pallas_call x1, Pallas kernels: 83.1 us -> 79.3 us  [main_call(): pl.pallas_call(functools.partial(main_kernel, steps), grid=(steps,), in_s...]
    pallas_call x1, Pallas kernels: 40.5 us -> 41.9 us  [front_call(): pl.pallas_call(functools.partial(front_kernel, tp, sp, steps), grid=(step...]
    pallas_call x1 -> x2, Pallas kernels: 11.4 us -> 11.9 us  [the longest x1 10.3 us: wgrad_call(): pl.pallas_call(functools.partial(wgrad_kernel, sp), in_specs=[pl.BlockSpe...]
where the time goes in v3:
time: 134 us
  Pallas kernels  133 us (99%)
    pallas_call x1, Pallas kernels, main_call(): pl.pallas_call(functools.partial(main_kernel, steps), grid=(steps,), in_s...  79.3 us
    pallas_call x1, Pallas kernels, front_call(): pl.pallas_call(functools.partial(front_kernel, tp, sp, steps), grid=(step...  41.9 us
    pallas_call x1, Pallas kernels, wgrad_call(): pl.pallas_call(functools.partial(wgrad_kernel, sp), in_specs=[pl.BlockSpe...  10.3 us

profile of v3, /device:TPU:97, one launch (start us, length us, event | category | flops | bytes accessed | tf_op | source)
XLA Modules:
  0.0 133.8 jit_solution(10956347205663935675)
XLA Ops:
  0.6 41.9 %front.1 = (bf16[384,16384]{1,0:T(8,128)(2,1)}, bf16[384,16384]{1,0:T(8,128)(2,1)}, f32[8,16384]{1,0:T(8,128)}, bf16[864,384]{1,0:T(8,128)(2,1)}, bf16[384,1152]...) custom-call(bf16[16384,384]{1,0:T(8,128)(2,1)} %x_ref.3, ...), custom_call_target="tpu_custom_call" | custom-call | flops 4831838208 | bytes 25165824 | tf_op jit(solution)/shard_map/front/pallas_call | solution.py:301
  42.5 79.3 %main.1 = (bf16[16384,384]{1,0:T(8,128)(2,1)}, bf16[16384,384]{1,0:T(8,128)(2,1)}, f32[8,56,384]{2,1,0:T(8,128)}) custom-call(bf16[16384,384]{1,0:T(8,128)(2,1)} %x_ref.3, bf16[16384,384]{1,0:T(8,128)(2,1)} %g_ref.3, bf16[384,16384]{1,0:T(8,128)(2,1)} %get-tuple-element.27.save_ref, bf16[384,16384]{1,0:T(8,128)(2,1)} %get-tuple-element.28.u_ref, ...), custom_call_target="tpu_custom_call" | custom-call | flops 43486543872 | bytes 50331648 | tf_op jit(solution)/shard_map/main/pallas_call | solution.py:456
  121.9 10.3 %wgrad.1.sum_ref = f32[56,384]{1,0:T(8,128)} custom-call(f32[8,56,384]{2,1,0:T(8,128)} %get-tuple-element.40.in_ref), custom_call_target="tpu_custom_call" | custom-call | tf_op jit(solution)/shard_map/wgrad/pallas_call | solution.py:519
  132.2 1.6 %finish.1 = (f32[3,48,96]{2,1,0:T(8,128)}, f32[12,384]{1,0:T(8,128)}, f32[384]{0:T(512)}, f32[384]{0:T(512)}, f32[8]{0:T(128)}) custom-call(f32[56,384]{1,0:T(8,128)} %wgrad.1.sum_ref, f32[1,128]{1,0:T(1,128)} %get-tuple-element.41.dt_ref), custom_call_target="tpu_custom_call" | custom-call | tf_op jit(solution)/shard_map/finish/pallas_call | solution.py:555

commit v4 on v3

--- a/solution.py
+++ b/solution.py
@@ -278,7 +278,7 @@
             c.wait()
 
 
-def front_call(x, g, w, w4, gam, bet, temps, tp, sp, block=2048):
+def front_call(x, g, w, w4, gam, bet, temps, tp, sp, block=4096):
     rows, d = x.shape
     own = w4.shape[0]
     head = d // temps.shape[0]

time: 134 us -> 133 us (level)
  no operation moved by 1% of the time
where the time goes in v4:
time: 133 us
  Pallas kernels  132 us (99%)
    pallas_call x1, Pallas kernels, main_call(): pl.pallas_call(functools.partial(main_kernel, steps), grid=(steps,), in_s...  79.3 us
    pallas_call x1, Pallas kernels, front_call(): pl.pallas_call(functools.partial(front_kernel, tp, sp, steps), grid=(step...  40.7 us
    pallas_call x1, Pallas kernels, wgrad_call(): pl.pallas_call(functools.partial(wgrad_kernel, sp), in_specs=[pl.BlockSpe...  10.3 us

profile of v4, /device:TPU:97, one launch (start us, length us, event | category | flops | bytes accessed | tf_op | source)
XLA Modules:
  0.0 132.7 jit_solution(15919276715830458353)
XLA Ops:
  0.6 40.7 %front.1 = (bf16[384,16384]{1,0:T(8,128)(2,1)}, bf16[384,16384]{1,0:T(8,128)(2,1)}, f32[8,16384]{1,0:T(8,128)}, bf16[864,384]{1,0:T(8,128)(2,1)}, bf16[384,1152]...) custom-call(bf16[16384,384]{1,0:T(8,128)(2,1)} %x_ref.3, ...), custom_call_target="tpu_custom_call" | custom-call | flops 4831838208 | bytes 25165824 | tf_op jit(solution)/shard_map/front/pallas_call | solution.py:301
  41.4 79.3 %main.1 = (bf16[16384,384]{1,0:T(8,128)(2,1)}, bf16[16384,384]{1,0:T(8,128)(2,1)}, f32[8,56,384]{2,1,0:T(8,128)}) custom-call(bf16[16384,384]{1,0:T(8,128)(2,1)} %x_ref.3, bf16[16384,384]{1,0:T(8,128)(2,1)} %g_ref.3, bf16[384,16384]{1,0:T(8,128)(2,1)} %get-tuple-element.27.save_ref, bf16[384,16384]{1,0:T(8,128)(2,1)} %get-tuple-element.28.u_ref, ...), custom_call_target="tpu_custom_call" | custom-call | flops 43486543872 | bytes 50331648 | tf_op jit(solution)/shard_map/main/pallas_call | solution.py:456
  120.7 10.3 %wgrad.1.sum_ref = f32[56,384]{1,0:T(8,128)} custom-call(f32[8,56,384]{2,1,0:T(8,128)} %get-tuple-element.40.in_ref), custom_call_target="tpu_custom_call" | custom-call | tf_op jit(solution)/shard_map/wgrad/pallas_call | solution.py:519
  131.0 1.6 %finish.1 = (f32[3,48,96]{2,1,0:T(8,128)}, f32[12,384]{1,0:T(8,128)}, f32[384]{0:T(512)}, f32[384]{0:T(512)}, f32[8]{0:T(128)}) custom-call(f32[56,384]{1,0:T(8,128)} %wgrad.1.sum_ref, f32[1,128]{1,0:T(1,128)} %get-tuple-element.41.dt_ref), custom_call_target="tpu_custom_call" | custom-call | tf_op jit(solution)/shard_map/finish/pallas_call | solution.py:555

commit v5 on v4

--- a/solution.py
+++ b/solution.py
@@ -57,7 +57,7 @@
     row = lax.broadcasted_iota(jnp.int32, (head, LANES), 0)
     valid = lane < head
     eye = lane == row
-    pick = lambda i: jnp.sum(jnp.where(lane == i, t, 0.0), axis=1, keepdims=True)
+    pick = lambda i: t[:, i : i + 1]
     q2 = pick(2 * head)
     k2 = jnp.sum(jnp.where(eye, pick(2 * head + 1), 0.0), axis=0, keepdims=True)
     k2 = jnp.where(valid, k2, 1.0)
@@ -162,27 +162,26 @@
             v = qkv[e * own : (e + 1) * own].astype(BF16)
             ref[r : r + own, at(n)] = v
             save_s[slot, e * own : (e + 1) * own, at(n)] = v
-            if e == 0:
+            if e < 2:
                 v = v.astype(F32)
                 v = v * v
-                sq[...] += v[:, :LANES] + v[:, LANES:]
+                sq[e * own : (e + 1) * own] += v[:, :LANES] + v[:, LANES:]
         v = dot(w4_ref[...], gt[:, at(n)]).astype(BF16)
         qd[own:, at(n)] = v
         save_s[slot, 3 * own :, at(n)] = v
 
     def gram(n):
-        cols = pl.ds(n * NT, 2 * NT)
-        left = jnp.concatenate([qd[:, cols], kv[0:own, cols]], axis=0)
-        acc[:, 0 : 2 * own] += dot_nt(left, kv[:, cols])
+        cols = pl.ds(n * NT, 4 * NT)
+        acc[:, 0 : 2 * own] += dot_nt(qd[:, cols], kv[:, cols])
 
     norm(0)
     for n in range(tiles):
         if n + 1 < tiles:
             norm(n + 1)
-        if n >= 2 and n % 2 == 0:
-            gram(n - 2)
+        if n >= 4 and n % 4 == 0:
+            gram(n - 4)
         project(n)
-    gram(tiles - 2)
+    gram(tiles - 4)
     for c in save_copies(step, slot):
         c.start()
 
@@ -200,7 +199,7 @@
         for h in range(2):
             r = h * head
             q2 = jnp.sum(sq[r : r + head, :], axis=1, keepdims=True)
-            k2 = jnp.sum(jnp.where(lane == row, block(2 * own + r, r, 0), 0.0), axis=1, keepdims=True)
+            k2 = jnp.sum(sq[own + r : own + r + head, :], axis=1, keepdims=True)
             v = jnp.where(valid, block(r, r, 0), block(own + r, own + r, head))
             v = jnp.where(lane == 2 * head, q2, v)
             sums[r : r + head, :] = jnp.where(lane == 2 * head + 1, k2, v)
@@ -242,20 +241,18 @@
                 )
         for c in copies:
             c.start()
-        for c in copies:
-            c.wait_send()
-        remote(state.at[0, core], state.at[0, 1 - core], send_b.at[0, 0], recv_b.at[0, 1 - core], other).wait_recv()
-        for k in range(1, tp):
-            for t in range(2):
-                remote(state.at[0, core], state.at[tp - k, t], send_b.at[k, t], recv_b.at[k, t], tp_peers[k - 1][t]).wait_recv()
-
         lane1 = lax.broadcasted_iota(jnp.int32, dt_ref.shape, 1)
         dt = jnp.zeros(dt_ref.shape, F32)
         zero = jnp.zeros((head, d - LANES), F32)
-        for j in range(tp):
+        for j in (0, tp - 1, 1, *range(2, tp - 1)):
+            k = tp - j
+            if j == 0:
+                remote(state.at[0, core], state.at[0, 1 - core], send_b.at[0, 0], recv_b.at[0, 1 - core], other).wait_recv()
             for h in range(2):
+                if j:
+                    remote(state.at[0, core], state.at[j, h], send_b.at[k, h], recv_b.at[k, h], tp_peers[k - 1][h]).wait_recv()
                 t = state[j, h]
-                pick = lambda i: jnp.sum(jnp.where(lane == i, t, 0.0), axis=1, keepdims=True)
+                pick = lambda i: t[:, i : i + 1]
                 r = j * own + h * head
                 att = jnp.concatenate([jnp.where(valid, t, 0.0), zero], axis=1)
                 d_gram = jnp.concatenate([jnp.where(valid, pltpu.roll(t, LANES - head, 1), 0.0), zero], axis=1)
@@ -265,6 +262,8 @@
                 ck_ref[r : r + head, :] = jnp.broadcast_to(pick(2 * head + 1), (head, NT))
                 which = lax.rem(my_tp + j, tp) * 2 + h
                 dt = jnp.where(lane1 == which, pick(2 * head + 2)[0:1, :], dt)
+        for c in copies:
+            c.wait_send()
         dt_ref[...] = dt
         low = m1_ref.shape[1]
         for i in range(2):
@@ -317,8 +316,8 @@
             pltpu.VMEM((2, d, block), BF16),
             pltpu.VMEM((2 * own, block), BF16),
             pltpu.VMEM((2 * own, block), BF16),
-            pltpu.VMEM((3 * own, 256), F32),
-            pltpu.VMEM((own, LANES), F32),
+            pltpu.VMEM((2 * own, 256), F32),
+            pltpu.VMEM((2 * own, LANES), F32),
             pltpu.VMEM((tp, 4, own, d), BF16),
             pltpu.VMEM((own, LANES), F32),
             pltpu.VMEM((head, LANES), F32),
@@ -386,8 +385,7 @@
             y_ref[at(n), c : c + m] = yt.astype(BF16).T
         gx[:, at(n)] = dot(wn[...], rt[:, at(n)])
 
-    def norm_bwd(first):
-        pair = (first, first + 1)
+    def norm_bwd(*pair):
         mean = {n: st_ref[0:1, at(n)] for n in pair}
         inv = {n: st_ref[1:2, at(n)] for n in pair}
         s1 = {n: jnp.zeros((8, NT), F32) for n in pair}
@@ -402,9 +400,9 @@
                 s2[n] = s2[n] + fold8(duh * gm)
                 sum_h.append(duh)
                 sum_u.append(du)
-            v = sum_h[0] + sum_h[1]
+            v = sum(sum_h[1:], sum_h[0])
             acc_g[0, c : c + CH, :] += v[:, :LANES] + v[:, LANES:]
-            v = sum_u[0] + sum_u[1]
+            v = sum(sum_u[1:], sum_u[0])
             acc_g[1, c : c + CH, :] += v[:, :LANES] + v[:, LANES:]
         for n in pair:
             m1_ = jnp.sum(s1[n], axis=0, keepdims=True) * (1.0 / d)
@@ -417,13 +415,15 @@
                 gt[c : c + CH, at(n)] = (v + gt[c : c + CH, at(n)].astype(F32)).astype(BF16)
             dx_ref[at(n), :] = gt[:, at(n)].T
 
-    stages = (project, mix, out)
-    for n in range(tiles + len(stages) + 1):
-        if n >= 4 and n % 2 == 0:
-            norm_bwd(n - 4)
-        for k in reversed(range(len(stages))):
-            if 0 <= n - k < tiles:
-                stages[k](n - k)
+    for n in range(tiles + 3):
+        if n >= 3:
+            norm_bwd(n - 3)
+        if n < tiles:
+            project(n)
+        if 2 <= n < tiles + 2:
+            out(n - 2)
+        if 1 <= n < tiles + 1:
+            mix(n - 1)
     r_own = jnp.concatenate([rt[e * d : e * d + own, :] for e in range(3)], axis=0)
     acc_w[...] += dot_nt(r_own, u_ref[...])
     acc_o[...] += dot(ot[0:own, :], g_ref[...])

time: 133 us -> 130 us (0.977)
  Pallas kernels: 132 us -> 129 us
    pallas_call x1, Pallas kernels: 79.3 us -> 77.9 us  [main_call(): pl.pallas_call(functools.partial(main_kernel, steps), grid=(steps,), in_s...]
where the time goes in v5:
time: 130 us
  Pallas kernels  129 us (99%)
    pallas_call x1, Pallas kernels, main_call(): pl.pallas_call(functools.partial(main_kernel, steps), grid=(steps,), in_s...  77.9 us
    pallas_call x1, Pallas kernels, front_call(): pl.pallas_call(functools.partial(front_kernel, tp, sp, steps), grid=(step...  40.1 us
    pallas_call x1, Pallas kernels, wgrad_call(): pl.pallas_call(functools.partial(wgrad_kernel, sp), in_specs=[pl.BlockSpe...  9.55 us

profile of v5, /device:TPU:97, one launch (start us, length us, event | category | flops | bytes accessed | tf_op | source)
XLA Modules:
  0.0 129.8 jit_solution(9041824467933937457)
XLA Ops:
  0.6 40.1 %front.1 = (bf16[384,16384]{1,0:T(8,128)(2,1)}, bf16[384,16384]{1,0:T(8,128)(2,1)}, f32[8,16384]{1,0:T(8,128)}, bf16[864,384]{1,0:T(8,128)(2,1)}, bf16[384,1152]...) custom-call(bf16[16384,384]{1,0:T(8,128)(2,1)} %x_ref.3, ...), custom_call_target="tpu_custom_call" | custom-call | flops 4831838208 | bytes 25165824 | tf_op jit(solution)/shard_map/front/pallas_call | solution.py:300
  40.8 77.9 %main.1 = (bf16[16384,384]{1,0:T(8,128)(2,1)}, bf16[16384,384]{1,0:T(8,128)(2,1)}, f32[8,56,384]{2,1,0:T(8,128)}) custom-call(bf16[16384,384]{1,0:T(8,128)(2,1)} %x_ref.3, bf16[16384,384]{1,0:T(8,128)(2,1)} %g_ref.3, bf16[384,16384]{1,0:T(8,128)(2,1)} %get-tuple-element.27.save_ref, bf16[384,16384]{1,0:T(8,128)(2,1)} %get-tuple-element.28.u_ref, ...), custom_call_target="tpu_custom_call" | custom-call | flops 43486543872 | bytes 50331648 | tf_op jit(solution)/shard_map/main/pallas_call | solution.py:456
  118.6 9.6 %wgrad.1.sum_ref = f32[56,384]{1,0:T(8,128)} custom-call(f32[8,56,384]{2,1,0:T(8,128)} %get-tuple-element.40.in_ref), custom_call_target="tpu_custom_call" | custom-call | tf_op jit(solution)/shard_map/wgrad/pallas_call | solution.py:519
  128.2 1.6 %finish.1 = (f32[3,48,96]{2,1,0:T(8,128)}, f32[12,384]{1,0:T(8,128)}, f32[384]{0:T(512)}, f32[384]{0:T(512)}, f32[8]{0:T(128)}) custom-call(f32[56,384]{1,0:T(8,128)} %wgrad.1.sum_ref, f32[1,128]{1,0:T(1,128)} %get-tuple-element.41.dt_ref), custom_call_target="tpu_custom_call" | custom-call | tf_op jit(solution)/shard_map/finish/pallas_call | solution.py:555

commit v6 on v5

--- a/solution.py
+++ b/solution.py
@@ -110,7 +110,6 @@
         spread_columns(bet_ref, bet)
         acc[...] = jnp.zeros_like(acc)
         sq[...] = jnp.zeros_like(sq)
-        big[...] = jnp.zeros_like(big)
 
     def weight_copies():
         out = []
@@ -217,6 +216,7 @@
         ]
         for c in copies:
             c.start()
+        big[...] = jnp.zeros_like(big)
         pieces = [(w_ref, w4_ref)] + [(wall.at[j, 0:3], wall.at[j, 3]) for j in range(1, tp)]
         for j, (piece, piece4) in enumerate(pieces):
             for e in range(3):
@@ -342,7 +342,7 @@
     )(x, g, w, w4, gam, bet, temps)
 
 
-def main_kernel(steps, x_ref, g_ref, save_ref, u_ref, st_ref, wt, wn, wo, wot, m1, m2, gam_ref, cq, ck, y_ref, dx_ref, dw_ref,
+def main_kernel(steps, x_ref, g_ref, save_ref, u_ref, st_ref, wt, wn, wo, wot, m1, m2, gam_ref, cq, ck, y_ref, dx_ref, dw_ref, gb_ref,
                 gam, xt, gt, qkv, do, ot, rt, gx, acc_w, acc_o, acc_g):
     step = pl.program_id(0)
     rows, d = x_ref.shape
@@ -430,7 +430,7 @@
 
     @pl.when(step == steps - 1)
     def _():
-        sp, slot_rows = dw_ref.shape[0], dw_ref.shape[1]
+        sp = dw_ref.shape[0]
         per = d // sp
         sub = own // sp
         wgrad = acc_w[...].T
@@ -438,10 +438,10 @@
             dw_ref[s, 0:per, 0 : 3 * own] = wgrad[s * per : (s + 1) * per, :]
             for q in range(d // own):
                 dw_ref[s, q * sub : (q + 1) * sub, 3 * own :] = acc_o[s * sub : (s + 1) * sub, q * own : (q + 1) * own]
-        zero = jnp.zeros((slot_rows - per - 2, d), F32)
-        gb = jnp.concatenate([jnp.sum(acc_g[i].T, axis=0, keepdims=True) for i in range(2)] + [zero], axis=0)
-        for s in range(sp):
-            dw_ref[s, per:slot_rows, :] = gb
+        for i in range(2):
+            row = jnp.sum(acc_g[i].T, axis=0, keepdims=True)
+            for q in range(d // own):
+                gb_ref[i * (d // own) + q : i * (d // own) + q + 1, 0:own] = row[:, q * own : (q + 1) * own]
 
 
 def main_call(x, g, save, u, st, wt, wn, wo, wot, m1, m2, gam, cq, ck, sp, block=2048):
@@ -451,14 +451,15 @@
     row = pl.BlockSpec((block, d), lambda i: (i, 0))
     col = lambda a: pl.BlockSpec((a.shape[0], block), lambda i: (0, i))
     full = lambda a: pl.BlockSpec(a.shape, lambda i: (0,) * a.ndim)
-    slot = (sp, d // sp + 8, d)
+    slot = (sp, d // sp, d)
+    sums = (2 * d // own, LANES)
     smalls = (wt, wn, wo, wot, m1, m2, gam, cq, ck)
     return pl.pallas_call(
         functools.partial(main_kernel, steps),
         grid=(steps,),
         in_specs=[row, row, col(save), col(u), col(st)] + [full(a) for a in smalls],
-        out_specs=[row, row, pl.BlockSpec(slot, lambda i: (0, 0, 0))],
-        out_shape=[jax.ShapeDtypeStruct((rows, d), BF16), jax.ShapeDtypeStruct((rows, d), BF16), jax.ShapeDtypeStruct(slot, F32)],
+        out_specs=[row, row, pl.BlockSpec(slot, lambda i: (0, 0, 0)), pl.BlockSpec(sums, lambda i: (0, 0))],
+        out_shape=[jax.ShapeDtypeStruct((rows, d), BF16), jax.ShapeDtypeStruct((rows, d), BF16), jax.ShapeDtypeStruct(slot, F32), jax.ShapeDtypeStruct(sums, F32)],
         scratch_shapes=[
             pltpu.VMEM((d, NT), F32),
             pltpu.VMEM((d, block), BF16),
@@ -478,87 +479,114 @@
     )(x, g, save, u, st, *smalls)
 
 
-def wgrad_kernel(sp, in_ref, out_ref, mine, pair, got, sem, send_a, recv_a, send_b, recv_b):
+def wgrad_kernel(sp, in_ref, gb_in, out_ref, gb_out, mine, pair, got, gb_mine, gb_pair, gb_got, sem, send_a, recv_a, send_b, recv_b):
     my = lax.axis_index("sp")
     chips = sp // 2
     core, chip = lax.rem(my, 2), my // 2
     other = {"sp": chip * 2 + 1 - core}
-    peers = [{"sp": lax.rem(chip + k, chips) * 2 + core} for k in range(1, chips)]
+    there = [lax.rem(chip + k, chips) for k in range(chips)]
+    peers = [{"sp": c * 2 + core} for c in there]
     barrier = pltpu.get_barrier_semaphore()
-    for peer in [other] + peers:
+    for peer in [other] + peers[1:]:
         pl.semaphore_signal(barrier, inc=1, device_id=peer, device_id_type=MESH)
-    load = pltpu.make_async_copy(in_ref, mine, sem)
-    load.start()
-    load.wait()
+    loads = [pltpu.make_async_copy(in_ref, mine, sem.at[0]), pltpu.make_async_copy(gb_in, gb_mine, sem.at[1])]
+    for c in loads:
+        c.start()
+    for c in loads:
+        c.wait()
     pl.semaphore_wait(barrier, chips)
-    first = [remote(mine.at[2 * c + 1 - core], pair.at[c], send_a.at[c], recv_a.at[c], other) for c in range(chips)]
-    for c in first:
+    order = sorted(range(1, chips), key=lambda k: -min(k, chips - k)) + [0]
+    first = [remote(mine.at[2 * c + 1 - core], pair.at[c], send_a.at[k], recv_a.at[k], other) for k, c in enumerate(there)]
+    gb_first = remote(gb_mine, gb_pair, send_a.at[chips], recv_a.at[chips], other)
+    for k in order:
+        first[k].start()
+    gb_first.start()
+    second = {
+        k: remote(got.at[chips + there[k]], got.at[chip], send_b.at[k], recv_b.at[k], peers[k]) for k in range(1, chips)
+    }
+    for k in order:
+        first[k].wait()
+        v = mine[2 * there[k] + core] + pair[there[k]]
+        if k:
+            got[chips + there[k]] = v
+            second[k].start()
+        else:
+            got[chip] = v
+    gb_first.wait()
+    gb_got[chips] = gb_mine[...] + gb_pair[...]
+    gb_second = [
+        remote(gb_got.at[chips], gb_got.at[chip], send_b.at[chips + k], recv_b.at[chips + k], peers[k]) for k in range(1, chips)
+    ]
+    for c in gb_second:
         c.start()
-    for c in range(chips):
-        first[c].wait()
-    for c in range(chips):
-        got[chips + c] = mine[2 * c + core] + pair[c]
-    second = [
-        remote(got.at[chips + lax.rem(chip + k, chips)], got.at[chip], send_b.at[k], recv_b.at[k], peers[k - 1])
-        for k in range(1, chips)
-    ]
-    for c in second:
-        c.start()
-    got[chip] = got[chips + chip]
-    for c in second:
-        c.wait()
+    gb_got[chip] = gb_mine[...] + gb_pair[...]
+    for k in order[:-1]:
+        second[k].wait()
     total = got[0]
     for c in range(1, chips):
         total = total + got[c]
     out_ref[...] = total
-
-
-def wgrad_call(parts):
+    for c in gb_second:
+        c.wait()
+    total = gb_got[0]
+    for c in range(1, chips):
+        total = total + gb_got[c]
+    gb_out[...] = total
+
+
+def wgrad_call(parts, gb):
     sp, slot = parts.shape[0], parts.shape[1:]
+    chips = sp // 2
     dma = pltpu.SemaphoreType.DMA
+    hbm, vmem = pl.BlockSpec(memory_space=pl.ANY), pl.BlockSpec(memory_space=pltpu.VMEM)
     return pl.pallas_call(
         functools.partial(wgrad_kernel, sp),
-        in_specs=[pl.BlockSpec(memory_space=pl.ANY)],
-        out_specs=pl.BlockSpec(memory_space=pltpu.VMEM),
-        out_shape=jax.ShapeDtypeStruct(slot, F32),
+        in_specs=[hbm, hbm],
+        out_specs=[vmem, vmem],
+        out_shape=[jax.ShapeDtypeStruct(slot, F32), jax.ShapeDtypeStruct(gb.shape, F32)],
         scratch_shapes=[
             pltpu.VMEM((sp, *slot), F32),
-            pltpu.VMEM((sp // 2, *slot), F32),
+            pltpu.VMEM((chips, *slot), F32),
             pltpu.VMEM((sp, *slot), F32),
-            dma,
-            dma((sp // 2,)),
-            dma((sp // 2,)),
-            dma((sp // 2,)),
-            dma((sp // 2,)),
+            pltpu.VMEM(gb.shape, F32),
+            pltpu.VMEM(gb.shape, F32),
+            pltpu.VMEM((chips + 1, *gb.shape), F32),
+            dma((2,)),
+            dma((chips + 1,)),
+            dma((chips + 1,)),
+            dma((sp,)),
+            dma((sp,)),
         ],
         compiler_params=pltpu.CompilerParams(collective_id=1, has_side_effects=True),
         name="wgrad",
-    )(parts)
-
-
-def finish_kernel(sum_ref, dt_ref, w_ref, o_ref, gam_ref, bet_ref, tau_ref):
-    per, own = w_ref.shape[1:]
+    )(parts, gb)
+
+
+def finish_kernel(sum_ref, gb_ref, dt_ref, w_ref, o_ref, gam_ref, bet_ref, tau_ref):
+    own = w_ref.shape[2]
     sub = o_ref.shape[0]
+    split = o_ref.shape[1] // own
     for e in range(3):
-        w_ref[e] = sum_ref[0:per, e * own : (e + 1) * own]
-    for q in range(o_ref.shape[1] // own):
+        w_ref[e] = sum_ref[:, e * own : (e + 1) * own]
+    for q in range(split):
         o_ref[:, q * own : (q + 1) * own] = sum_ref[q * sub : (q + 1) * sub, 3 * own :]
-    gam_ref[...] = sum_ref[per]
-    bet_ref[...] = sum_ref[per + 1]
+    for i, ref in enumerate((gam_ref, bet_ref)):
+        row = [gb_ref[i * split + q : i * split + q + 1, 0:own] for q in range(split)]
+        ref[...] = jnp.concatenate(row, axis=1)[0]
     tau_ref[...] = dt_ref[0, 0 : tau_ref.shape[0]]
 
 
-def finish_call(total, dt, own, sp, heads):
+def finish_call(total, gb, dt, own, sp, heads):
     d = total.shape[1]
     vmem = pl.BlockSpec(memory_space=pltpu.VMEM)
     shapes = [(3, d // sp, own), (own // sp, d), (d,), (d,), (heads,)]
     return pl.pallas_call(
         finish_kernel,
-        in_specs=[vmem, vmem],
+        in_specs=[vmem] * 3,
         out_specs=[vmem] * 5,
         out_shape=[jax.ShapeDtypeStruct(s, F32) for s in shapes],
         name="finish",
-    )(total, dt)
+    )(total, gb, dt)
 
 
 def solution(mesh):
@@ -569,9 +597,9 @@
         save, u, st, wt, wn, wo, wot, m1, m2, cq, ck, dt = front_call(
             x, g, w_qkv.transpose(1, 2, 0), w_out, gamma, beta, temps, tp, sp
         )
-        y, dx, parts = main_call(x, g, save, u, st, wt, wn, wo, wot, m1, m2, gamma, cq, ck, sp)
+        y, dx, parts, gb = main_call(x, g, save, u, st, wt, wn, wo, wot, m1, m2, gamma, cq, ck, sp)
         grad_w, grad_o, grad_gamma, grad_beta, grad_temp = finish_call(
-            wgrad_call(parts), dt, w_out.shape[0], sp, temps.shape[0]
+            *wgrad_call(parts, gb), dt, w_out.shape[0], sp, temps.shape[0]
         )
         return y, dx, grad_w.transpose(1, 0, 2), grad_o, grad_gamma, grad_beta, grad_temp
 

time: 130 us -> 129 us (level)
  no operation moved by 1% of the time
where the time goes in v6:
time: 129 us
  Pallas kernels  128 us (99%)
    pallas_call x1, Pallas kernels, main_call(): pl.pallas_call(functools.partial(main_kernel, steps), grid=(steps,), in_s...  77.9 us
    pallas_call x1, Pallas kernels, front_call(): pl.pallas_call(functools.partial(front_kernel, tp, sp, steps), grid=(step...  40.2 us
    pallas_call x1, Pallas kernels, wgrad_call(): pl.pallas_call(functools.partial(wgrad_kernel, sp), in_specs=[hbm, hbm],...  8.81 us

profile of v6, /device:TPU:97, one launch (start us, length us, event | category | flops | bytes accessed | tf_op | source)
XLA Modules:
  0.0 129.1 jit_solution(6585891733570322522)
XLA Ops:
  0.6 40.2 %front.1 = (bf16[384,16384]{1,0:T(8,128)(2,1)}, bf16[384,16384]{1,0:T(8,128)(2,1)}, f32[8,16384]{1,0:T(8,128)}, bf16[864,384]{1,0:T(8,128)(2,1)}, bf16[384,1152]...) custom-call(bf16[16384,384]{1,0:T(8,128)(2,1)} %x_ref.3, ...), custom_call_target="tpu_custom_call" | custom-call | flops 4831838208 | bytes 25165824 | tf_op jit(solution)/shard_map/front/pallas_call | solution.py:300
  40.8 77.9 %main.1 = (bf16[16384,384]{1,0:T(8,128)(2,1)}, bf16[16384,384]{1,0:T(8,128)(2,1)}, f32[8,48,384]{2,1,0:T(8,128)}, f32[8,128]{1,0:T(8,128)}) custom-call(bf16[16384,384]{1,0:T(8,128)(2,1)} %x_ref.3, bf16[16384,384]{1,0:T(8,128)(2,1)} %g_ref.3, bf16[384,16384]{1,0:T(8,128)(2,1)} %get-tuple-element.30.save_ref, bf16[384,16384]{1,0:T(8,128)(2,1)} %get-tuple-element.31.u_ref, ...), custom_call_target="tpu_custom_call" | custom-call | flops 43486543872 | bytes 50331648 | tf_op jit(solution)/shard_map/main/pallas_call | solution.py:457
  118.7 8.8 %wgrad.1 = (f32[48,384]{1,0:T(8,128)}, f32[8,128]{1,0:T(8,128)}) custom-call(f32[8,48,384]{2,1,0:T(8,128)} %get-tuple-element.43.in_ref, f32[8,128]{1,0:T(8,128)} %get-tuple-element.44.gb_in), custom_call_target="tpu_custom_call" | custom-call | tf_op jit(solution)/shard_map/wgrad/pallas_call | solution.py:542
  127.5 1.6 %finish.1 = (f32[3,48,96]{2,1,0:T(8,128)}, f32[12,384]{1,0:T(8,128)}, f32[384]{0:T(512)}, f32[384]{0:T(512)}, f32[8]{0:T(128)}) custom-call(f32[48,384]{1,0:T(8,128)} %get-tuple-element.45.sum_ref, f32[8,128]{1,0:T(8,128)} %get-tuple-element.46.gb_ref, f32[1,128]{1,0:T(1,128)} %get-tuple-element.47.dt_ref), custom_call_target="tpu_custom_call" | custom-call | tf_op jit(solution)/shard_map/finish/pallas_call | solution.py:583

commit v7 on v6

--- a/solution.py
+++ b/solution.py
@@ -29,16 +29,15 @@
 
 def ln_stats(xt, cols):
     d = xt.shape[0]
-    shift = xt[0:16, cols].astype(F32)[0:1, :]
-    s1 = jnp.zeros((8, NT), F32)
-    s2 = jnp.zeros((8, NT), F32)
+    acc = jnp.zeros((8, NT), F32)
     for c in range(0, d, CH):
-        v = xt[c : c + CH, cols].astype(F32) - shift
-        s1 = s1 + fold8(v)
-        s2 = s2 + fold8(v * v)
-    off = jnp.sum(s1, axis=0, keepdims=True) * (1.0 / d)
-    var = jnp.sum(s2, axis=0, keepdims=True) * (1.0 / d) - off * off
-    return shift + off, lax.rsqrt(jnp.maximum(var, 0.0) + LN_EPS)
+        acc = acc + fold8(xt[c : c + CH, cols].astype(F32))
+    mean = jnp.sum(acc, axis=0, keepdims=True) * (1.0 / d)
+    acc = jnp.zeros((8, NT), F32)
+    for c in range(0, d, CH):
+        v = xt[c : c + CH, cols].astype(F32) - mean
+        acc = acc + fold8(v * v)
+    return mean, lax.rsqrt(jnp.sum(acc, axis=0, keepdims=True) * (1.0 / d) + LN_EPS)
 
 
 def spread_columns(row_ref, out):
@@ -146,11 +145,10 @@
         xt[:, at(n)] = x_ref[at(n), :].T
         gt[:, at(n)] = g_ref[at(n), :].T
         mean, inv = ln_stats(xt, at(n))
-        mean = mean * inv
         st_ref[0:1, at(n)] = mean
         st_ref[1:2, at(n)] = inv
         for c in range(0, d, CH):
-            v = xt[c : c + CH, at(n)].astype(F32) * inv - mean
+            v = (xt[c : c + CH, at(n)].astype(F32) - mean) * inv
             v = (v * gam[c : c + CH, :] + bet[c : c + CH, :]).astype(BF16)
             ut[c : c + CH, at(n)] = v
             u_s[slot, c : c + CH, at(n)] = v
@@ -395,7 +393,7 @@
             sum_h, sum_u = [], []
             for n in pair:
                 du = gx[c : c + CH, at(n)]
-                duh = du * (xt[c : c + CH, at(n)].astype(F32) * inv[n] - mean[n])
+                duh = du * ((xt[c : c + CH, at(n)].astype(F32) - mean[n]) * inv[n])
                 s1[n] = s1[n] + fold8(du * gm)
                 s2[n] = s2[n] + fold8(duh * gm)
                 sum_h.append(duh)
@@ -408,10 +406,10 @@
             m1_ = jnp.sum(s1[n], axis=0, keepdims=True) * (1.0 / d)
             m2_ = jnp.sum(s2[n], axis=0, keepdims=True) * (1.0 / d)
             slope = m2_ * inv[n] * inv[n]
-            base = inv[n] * (mean[n] * m2_ - m1_)
+            base = inv[n] * m1_
             gt[:, at(n)] = g_ref[at(n), :].T
             for c in range(0, d, CH):
-                v = gx[c : c + CH, at(n)] * gam[c : c + CH, :] * inv[n] + base - xt[c : c + CH, at(n)].astype(F32) * slope
+                v = gx[c : c + CH, at(n)] * gam[c : c + CH, :] * inv[n] - base - (xt[c : c + CH, at(n)].astype(F32) - mean[n]) * slope
                 gt[c : c + CH, at(n)] = (v + gt[c : c + CH, at(n)].astype(F32)).astype(BF16)
             dx_ref[at(n), :] = gt[:, at(n)].T
 

time: 129 us -> 131 us (1.016)
  Pallas kernels: 128 us -> 130 us
where the time goes in v7:
time: 131 us
  Pallas kernels  130 us (99%)
    pallas_call x1, Pallas kernels, main_call(): pl.pallas_call(functools.partial(main_kernel, steps), grid=(steps,), in_s...  78.6 us
    pallas_call x1, Pallas kernels, front_call(): pl.pallas_call(functools.partial(front_kernel, tp, sp, steps), grid=(step...  40.8 us
    pallas_call x1, Pallas kernels, wgrad_call(): pl.pallas_call(functools.partial(wgrad_kernel, sp), in_specs=[hbm, hbm],...  9.34 us

profile of v7, /device:TPU:97, one launch (start us, length us, event | category | flops | bytes accessed | tf_op | source)
XLA Modules:
  0.0 131.0 jit_solution(8204510477304249578)
XLA Ops:
  0.6 40.8 %front.1 = (bf16[384,16384]{1,0:T(8,128)(2,1)}, bf16[384,16384]{1,0:T(8,128)(2,1)}, f32[8,16384]{1,0:T(8,128)}, bf16[864,384]{1,0:T(8,128)(2,1)}, bf16[384,1152]...) custom-call(bf16[16384,384]{1,0:T(8,128)(2,1)} %x_ref.3, ...), custom_call_target="tpu_custom_call" | custom-call | flops 4831838208 | bytes 25165824 | tf_op jit(solution)/shard_map/front/pallas_call | solution.py:298
  41.4 78.6 %main.1 = (bf16[16384,384]{1,0:T(8,128)(2,1)}, bf16[16384,384]{1,0:T(8,128)(2,1)}, f32[8,48,384]{2,1,0:T(8,128)}, f32[8,128]{1,0:T(8,128)}) custom-call(bf16[16384,384]{1,0:T(8,128)(2,1)} %x_ref.3, bf16[16384,384]{1,0:T(8,128)(2,1)} %g_ref.3, bf16[384,16384]{1,0:T(8,128)(2,1)} %get-tuple-element.30.save_ref, bf16[384,16384]{1,0:T(8,128)(2,1)} %get-tuple-element.31.u_ref, ...), custom_call_target="tpu_custom_call" | custom-call | flops 43486543872 | bytes 50331648 | tf_op jit(solution)/shard_map/main/pallas_call | solution.py:455
  120.0 9.3 %wgrad.1 = (f32[48,384]{1,0:T(8,128)}, f32[8,128]{1,0:T(8,128)}) custom-call(f32[8,48,384]{2,1,0:T(8,128)} %get-tuple-element.43.in_ref, f32[8,128]{1,0:T(8,128)} %get-tuple-element.44.gb_in), custom_call_target="tpu_custom_call" | custom-call | tf_op jit(solution)/shard_map/wgrad/pallas_call | solution.py:540
  129.3 1.6 %finish.1 = (f32[3,48,96]{2,1,0:T(8,128)}, f32[12,384]{1,0:T(8,128)}, f32[384]{0:T(512)}, f32[384]{0:T(512)}, f32[8]{0:T(128)}) custom-call(f32[48,384]{1,0:T(8,128)} %get-tuple-element.45.sum_ref, f32[8,128]{1,0:T(8,128)} %get-tuple-element.46.gb_ref, f32[1,128]{1,0:T(1,128)} %get-tuple-element.47.dt_ref), custom_call_target="tpu_custom_call" | custom-call | tf_op jit(solution)/shard_map/finish/pallas_call | solution.py:581

commit v8 on v7

--- a/solution.py
+++ b/solution.py
@@ -406,10 +406,10 @@
             m1_ = jnp.sum(s1[n], axis=0, keepdims=True) * (1.0 / d)
             m2_ = jnp.sum(s2[n], axis=0, keepdims=True) * (1.0 / d)
             slope = m2_ * inv[n] * inv[n]
-            base = inv[n] * m1_
+            base = mean[n] * slope - inv[n] * m1_
             gt[:, at(n)] = g_ref[at(n), :].T
             for c in range(0, d, CH):
-                v = gx[c : c + CH, at(n)] * gam[c : c + CH, :] * inv[n] - base - (xt[c : c + CH, at(n)].astype(F32) - mean[n]) * slope
+                v = gx[c : c + CH, at(n)] * gam[c : c + CH, :] * inv[n] + base - xt[c : c + CH, at(n)].astype(F32) * slope
                 gt[c : c + CH, at(n)] = (v + gt[c : c + CH, at(n)].astype(F32)).astype(BF16)
             dx_ref[at(n), :] = gt[:, at(n)].T
 

time: 131 us -> 130 us (level)
    pallas_call x1, Pallas kernels: 78.6 us -> 77 us  [main_call(): pl.pallas_call(functools.partial(main_kernel, steps), grid=(steps,), in_s...]
where the time goes in v8:
time: 130 us; the launch traced here: 129 us
  Pallas kernels  129 us (99%)
    pallas_call x1, Pallas kernels, main_call(): pl.pallas_call(functools.partial(main_kernel, steps), grid=(steps,), in_s...  77 us
    pallas_call x1, Pallas kernels, front_call(): pl.pallas_call(functools.partial(front_kernel, tp, sp, steps), grid=(step...  40.8 us
    pallas_call x1, Pallas kernels, wgrad_call(): pl.pallas_call(functools.partial(wgrad_kernel, sp), in_specs=[hbm, hbm],...  9.35 us

profile of v8, /device:TPU:97, one launch (start us, length us, event | category | flops | bytes accessed | tf_op | source)
XLA Modules:
  0.0 129.4 jit_solution(11596305650826154856)
XLA Ops:
  0.6 40.8 %front.1 = (bf16[384,16384]{1,0:T(8,128)(2,1)}, bf16[384,16384]{1,0:T(8,128)(2,1)}, f32[8,16384]{1,0:T(8,128)}, bf16[864,384]{1,0:T(8,128)(2,1)}, bf16[384,1152]...) custom-call(bf16[16384,384]{1,0:T(8,128)(2,1)} %x_ref.3, ...), custom_call_target="tpu_custom_call" | custom-call | flops 4831838208 | bytes 25165824 | tf_op jit(solution)/shard_map/front/pallas_call | solution.py:298
  41.4 77.0 %main.1 = (bf16[16384,384]{1,0:T(8,128)(2,1)}, bf16[16384,384]{1,0:T(8,128)(2,1)}, f32[8,48,384]{2,1,0:T(8,128)}, f32[8,128]{1,0:T(8,128)}) custom-call(bf16[16384,384]{1,0:T(8,128)(2,1)} %x_ref.3, bf16[16384,384]{1,0:T(8,128)(2,1)} %g_ref.3, bf16[384,16384]{1,0:T(8,128)(2,1)} %get-tuple-element.30.save_ref, bf16[384,16384]{1,0:T(8,128)(2,1)} %get-tuple-element.31.u_ref, ...), custom_call_target="tpu_custom_call" | custom-call | flops 43486543872 | bytes 50331648 | tf_op jit(solution)/shard_map/main/pallas_call | solution.py:455
  118.4 9.3 %wgrad.1 = (f32[48,384]{1,0:T(8,128)}, f32[8,128]{1,0:T(8,128)}) custom-call(f32[8,48,384]{2,1,0:T(8,128)} %get-tuple-element.43.in_ref, f32[8,128]{1,0:T(8,128)} %get-tuple-element.44.gb_in), custom_call_target="tpu_custom_call" | custom-call | tf_op jit(solution)/shard_map/wgrad/pallas_call | solution.py:540
  127.8 1.6 %finish.1 = (f32[3,48,96]{2,1,0:T(8,128)}, f32[12,384]{1,0:T(8,128)}, f32[384]{0:T(512)}, f32[384]{0:T(512)}, f32[8]{0:T(128)}) custom-call(f32[48,384]{1,0:T(8,128)} %get-tuple-element.45.sum_ref, f32[8,128]{1,0:T(8,128)} %get-tuple-element.46.gb_ref, f32[1,128]{1,0:T(1,128)} %get-tuple-element.47.dt_ref), custom_call_target="tpu_custom_call" | custom-call | tf_op jit(solution)/shard_map/finish/pallas_call | solution.py:581
